TPU v7x, 32 devices: a whole 2x2x4 slice. The times are simulated.
32 devices in a mesh: gx: 4 (over y, x), gy: 8 (over z, core).
Axes of the slice: x: 2, y: 2, z: 4, core: 2. Of those that a mesh axis runs over, the one named last changes fastest.
Arguments:
- q_nodes: bfloat16 [32, 512, 4096], P(('gx', 'gy')), may hold values from -30 to 30, as said below
- k_cache: bfloat16 [32, 1024, 512], P(('gx', 'gy')), may hold values from -6 to 6, as said below
- v_cache: bfloat16 [32, 1024, 512], P(('gx', 'gy')), may hold values from -6 to 6
- k_tree: bfloat16 [32, 512, 512], P(('gx', 'gy')), may hold values from -6 to 6
- v_tree: bfloat16 [32, 512, 512], P(('gx', 'gy')), may hold values from -6 to 6
- anc_bits: int32 [32, 512, 16], P(('gx', 'gy')), may hold values from -2147483648 to 2147483647, as said below
- node_count: int32 [32], P(('gx', 'gy')), may hold values from 1 to 512, as said below
- cache_len: int32 [32], P(('gx', 'gy')), may hold values from 256 to 1024, as said below
- sinks: float32 [64], replicated, may hold values from 5 to 10
- o_weight: bfloat16 [4096, 2880], P(('gx', 'gy')), may hold values from -0.09375 to 0.09375
Outputs:
- attended: bfloat16 [32, 512, 4096], P(('gx', 'gy'))
- projected: bfloat16 [32, 512, 2880], P(('gx', 'gy'))
Inputs may be any that keep to these rules, and one draw needn't show every extreme that they name: `q_nodes`: custom draw of queries. `k_cache`: custom draw of keys. `anc_bits`: bit j mod 32 of word j // 32 in row i is set exactly when tree node j is node i or one of its ancestors; node 0 is the root and a node's ancestors have lower indices. `node_count`: write request r as a * 8 + b with b < 8. Where a + b is even, the tree has more than (2) * 128 nodes; elsewhere it has at most 128. Request 0 has 512 nodes. `cache_len`: request 0 has 1024 cached positions.
All inputs are finite; a program needn't handle non-finite values.
Results may differ from a plain program's by a relative error of at most 0.0055.
Values may be sent and summed in bfloat16 or wider, within the bound.
No kernel may reach another device: no remote copies, remote signals or barrier semaphores. Data moves between devices by JAX's collectives and lax.ppermute only.
A program may use at most 192 MiB of HBM per device.

v0:
```python
import jax
import jax.numpy as jnp
from jax import lax
from jax.sharding import PartitionSpec as P

QH = 64
KVH = 8
HD = 64
BLK = 128


MASKED = -1e30


def passed_along(x, axis, by):
    length = lax.axis_size(axis)
    return lax.ppermute(x, axis, [(i, (i + by) % length) for i in range(length)])


def unpack_bits(bit_words):
    shift_ids = jnp.arange(32, dtype=jnp.int32)
    bit_flags = jnp.bitwise_and(jnp.right_shift(bit_words[:, :, None], shift_ids), 1)
    return bit_flags.reshape(bit_words.shape[0], bit_words.shape[1] * 32) > 0


def attend_rows(
    q_rows, tree_ok, cache_keys, cache_values, tree_keys, tree_values, cache_count, sinks
):
    row_total = q_rows.shape[0]
    groups = QH // KVH
    head_width = groups * HD
    scale_factor = HD ** (-0.5)
    cache_ok = jnp.arange(cache_keys.shape[0], dtype=jnp.int32) < cache_count
    tree_mask = jnp.repeat(tree_ok, groups, axis=0)

    def per_kv_head(kv_head):
        q_part = lax.dynamic_slice_in_dim(q_rows, kv_head * head_width, head_width, 1).reshape(
            row_total * groups, HD
        )
        key_cache = lax.dynamic_slice_in_dim(cache_keys, kv_head * HD, HD, 1)
        value_cache = lax.dynamic_slice_in_dim(cache_values, kv_head * HD, HD, 1)
        key_tree = lax.dynamic_slice_in_dim(tree_keys, kv_head * HD, HD, 1)
        value_tree = lax.dynamic_slice_in_dim(tree_values, kv_head * HD, HD, 1)
        score_cache = (
            jnp.dot(q_part, key_cache.T, preferred_element_type=jnp.float32) * scale_factor
        )
        score_cache = jnp.where(cache_ok[None, :], score_cache, MASKED)
        score_tree = jnp.dot(q_part, key_tree.T, preferred_element_type=jnp.float32) * scale_factor
        score_tree = jnp.where(tree_mask, score_tree, MASKED)
        sink_rows = jnp.tile(
            lax.dynamic_slice_in_dim(sinks, kv_head * groups, groups, 0), row_total
        )
        row_max = jnp.maximum(
            sink_rows, jnp.maximum(jnp.max(score_cache, axis=1), jnp.max(score_tree, axis=1))
        )
        weight_cache = jnp.exp(score_cache - row_max[:, None])
        weight_tree = jnp.exp(score_tree - row_max[:, None])
        denominator = (
            jnp.exp(sink_rows - row_max)
            + jnp.sum(weight_cache, axis=1)
            + jnp.sum(weight_tree, axis=1)
        )
        numerator = jnp.dot(
            weight_cache.astype(jnp.bfloat16), value_cache, preferred_element_type=jnp.float32
        )
        numerator = numerator + jnp.dot(
            weight_tree.astype(jnp.bfloat16), value_tree, preferred_element_type=jnp.float32
        )
        return (numerator / denominator[:, None]).reshape(row_total, head_width)

    per_head = lax.map(per_kv_head, jnp.arange(KVH, dtype=jnp.int32))
    return jnp.transpose(per_head, (1, 0, 2)).reshape(row_total, QH * HD)


def on_device(
    q_nodes, k_cache, v_cache, k_tree, v_tree, anc_bits, node_count, cache_len, sinks, o_weight
):
    queries = q_nodes[0]
    cache_keys = k_cache[0]
    cache_values = v_cache[0]
    tree_keys = k_tree[0]
    tree_values = v_tree[0]
    bit_words = anc_bits[0]
    node_limit = node_count[0]
    cache_count = cache_len[0]
    node_total = queries.shape[0]
    block_size = BLK
    block_count = node_total // block_size
    live_blocks = (node_limit + block_size - 1) // block_size

    def home_step(block_index, result):
        row_start = block_index * block_size
        q_rows = lax.dynamic_slice_in_dim(queries, row_start, block_size, 0)
        bit_rows = lax.dynamic_slice_in_dim(bit_words, row_start, block_size, 0)
        rows_out = attend_rows(
            q_rows,
            unpack_bits(bit_rows),
            cache_keys,
            cache_values,
            tree_keys,
            tree_values,
            cache_count,
            sinks,
        )
        return lax.dynamic_update_slice_in_dim(result, rows_out.astype(jnp.bfloat16), row_start, 0)

    result = jnp.zeros_like(queries)
    send_x = (live_blocks >= block_count - 1).astype(jnp.int32)
    send_y = (live_blocks >= block_count).astype(jnp.int32)
    kept_blocks = live_blocks - send_x - send_y
    start_x = jnp.minimum(kept_blocks, block_count - 1) * block_size
    start_y = jnp.minimum(kept_blocks + send_x, block_count - 1) * block_size
    tree_rows_x = (block_count - 1) * block_size

    def make_parcel(row_start, is_moved, tree_rows):
        q_rows = lax.dynamic_slice_in_dim(queries, row_start, block_size, 0)
        bit_rows = lax.dynamic_slice_in_dim(bit_words, row_start, block_size, 0)
        header = jnp.stack([is_moved, cache_count])
        return (
            q_rows,
            bit_rows,
            cache_keys,
            cache_values,
            tree_keys[:tree_rows],
            tree_values[:tree_rows],
            header,
        )

    def attend_moved(parcel):
        q_rows, bit_rows, moved_keys, moved_values, moved_tree_keys, moved_tree_values, header = (
            parcel
        )

        def compute_block():
            tree_ok = unpack_bits(bit_rows)[:, : moved_tree_keys.shape[0]]
            return attend_rows(
                q_rows,
                tree_ok,
                moved_keys,
                moved_values,
                moved_tree_keys,
                moved_tree_values,
                header[1],
                sinks,
            ).astype(jnp.bfloat16)

        def empty_block():
            return jnp.zeros((block_size, QH * HD), jnp.bfloat16)

        return lax.cond(header[0] > 0, compute_block, empty_block)

    def put_back(result, rows_out, row_start, is_moved):
        current = lax.dynamic_slice_in_dim(result, row_start, block_size, 0)
        chosen_rows = jnp.where(is_moved > 0, rows_out, current)
        return lax.dynamic_update_slice_in_dim(result, chosen_rows, row_start, 0)

    parcel_x = make_parcel(start_x, send_x, tree_rows_x)
    parcel_y = make_parcel(start_y, send_y, node_total)
    got_x = passed_along(
        (parcel_x[0], parcel_x[1], parcel_x[2], parcel_x[3], parcel_x[4], parcel_x[5], parcel_x[6]),
        "gx",
        1,
    )
    got_y = passed_along(
        (parcel_y[0], parcel_y[1], parcel_y[2], parcel_y[3], parcel_y[4], parcel_y[5], parcel_y[6]),
        "gy",
        1,
    )
    result = lax.fori_loop(0, kept_blocks, home_step, result)
    done_x = attend_moved(got_x)
    done_y = attend_moved(got_y)
    returned_x = passed_along(done_x, "gx", -1)
    returned_y = passed_along(done_y, "gy", -1)
    result = put_back(result, returned_x, start_x, send_x)
    result = put_back(result, returned_y, start_y, send_y)
    node_live = jnp.arange(node_total, dtype=jnp.int32) < node_limit
    attended = jnp.where(node_live[:, None], result, jnp.zeros_like(result))
    projected = jnp.dot(
        attended,
        lax.all_gather(o_weight, ("gx", "gy"), axis=0, tiled=True),
        preferred_element_type=jnp.float32,
    )
    return (attended[None], projected.astype(jnp.bfloat16)[None])


def solution(mesh):
    placed = (
        P(("gx", "gy"), None, None),
        P(("gx", "gy"), None, None),
        P(("gx", "gy"), None, None),
        P(("gx", "gy"), None, None),
        P(("gx", "gy"), None, None),
        P(("gx", "gy"), None, None),
        P(("gx", "gy")),
        P(("gx", "gy")),
        P(),
        P(("gx", "gy"), None),
    )
    return jax.shard_map(
        on_device,
        mesh=mesh,
        in_specs=placed,
        out_specs=(P(("gx", "gy"), None, None), P(("gx", "gy"), None, None)),
        check_vma=False,
    )
```

profile of v0, /device:TPU:9, one launch (start us, length us, event | category | flops | bytes accessed | tf_op | source)
XLA Modules:
  0.0 603.9 jit_solution(9022590389764629002)
XLA Ops:
  17.5 71.7 %collective-permute-done = s32[2]{0:T(128)S(1)} collective-permute-done((s32[2]{0:T(128)S(1)}, s32[2]{0:T(128)S(1)}, u32[]{:S(2)}, u32[]{:S(2)}) %collective-permute-start) | collective-permute-done | bytes 40 | tf_op jit(solution)/shard_map/ppermute | solution.py:17
  89.3 3.3 collective-permute-done.1
  92.6 3.8 collective-permute-start.12
  97.5 13.3 %collective-permute-done.6 = bf16[384,512]{1,0:T(8,128)(2,1)} collective-permute-done((bf16[384,512]{1,0:T(8,128)(2,1)S(1)}, bf16[384,512]{1,0:T(8,128)(2,1)}, u32[]{:S(2)}, u32[]{:S(2)}) %collective-permute-start.6) | collective-permute-done | bytes 393248 | tf_op jit(solution)/shard_map/ppermute | solution.py:17
  113.1 144.6 %conditional.2 = (bf16[128,4096]{1,0:T(8,128)(2,1)}) conditional(s32[]{:T(128)} %bitcast.17, () %tuple.37, (s32[2]{0:T(128)S(1)}, s32[128,16]{0,1:T(8,128)S(1)}, bf16[128,4096]{1,0:T(8,128)(2,1)}, bf16[1024,512]{1,0:T(8,128)(2,1)S(1)}, f32[64]{0:T(128)S(1)}, /*index=5*/bf16[384,512]{1,0:T(8,128)(2,1)}, bf16[1024,512]{1,0:T(8,128)(2,1)}, ...), branch_computations={%region_8.9_spmd, %region_9.16_spmd} | conditional | flops 383731712 | bytes 41591464 | solution.py:150
  114.1 141.2 %while.41 = (s32[]{:T(128)}, bf16[8,128,512]{2,1,0:T(8,128)(2,1)}, s32[8]{0:T(128)S(1)}, bf16[128,4096]{1,0:T(8,128)(2,1)}, bf16[1024,512]{1,0:T(8,128)(2,1)S(1)...) while((s32[]{:T(128)}, bf16[8,128,512]{2,1,0:T(8,128)(2,1)}, ...), condition=%wide.region_15.15_spmd.clone, body=%wide.region_10.14_spmd.clone.sunk | while | flops 383584256 | bytes 38872024 | solution.py:71
  158.8 3.4 fusion.169
  176.5 3.5 fusion.169
  194.3 3.4 fusion.169
  212.0 3.3 fusion.169
  261.5 147.6 %while.44 = (s32[]{:T(128)}, bf16[512,4096]{1,0:T(8,128)(2,1)}, s32[]{:T(128)}, bf16[512,4096]{1,0:T(8,128)(2,1)}, s32[]{:T(128)}, /*index=5*/s32[512,16]{0,1:T(...) while((s32[]{:T(128)}, bf16[512,4096]{1,0:T(8,128)(2,1)}, ...), condition=%wide.region_7.8_spmd, body=%wide.region_0.7_spmd.sunk | while | flops 418252800 | bytes 47441316 | solution.py:169
  263.4 143.3 %while.45 = (s32[]{:T(128)}, bf16[8,128,512]{2,1,0:T(8,128)(2,1)}, s32[8]{0:T(128)S(1)}, bf16[128,4096]{1,0:T(8,128)(2,1)S(1)}, bf16[1024,512]{1,0:T(8,128)(2,1)...) while((s32[]{:T(128)}, bf16[8,128,512]{2,1,0:T(8,128)(2,1)}, ...), condition=%wide.region_6.6_spmd.clone, body=%wide.region_1.5_spmd.clone.sunk | while | flops 418056192 | bytes 40920024 | solution.py:71
  266.3 3.7 fusion.141
  284.2 3.7 fusion.141
  302.1 3.7 fusion.141
  320.0 3.7 fusion.141
  337.9 3.7 fusion.141
  355.8 3.7 fusion.141
  373.7 3.7 fusion.141
  391.6 3.7 fusion.141
  409.8 147.2 %collective-permute-start.15 = (bf16[128,4096]{1,0:T(8,128)(2,1)S(1)}, bf16[128,4096]{1,0:T(8,128)(2,1)S(1)}, u32[]{:S(2)}, u32[]{:S(2)}) collective-permute-start(bf16[128,4096]{1,0:T(8,128)(2,1)S(1)} %get-tuple-element.1063), channel_id=1, source_target_pairs={{0,7},{1,0},{2,1},{3,2},{4,3},{5,4},{6,5},{7,6},{8,15},{9,8},{10,9... | collective-permute-start | bytes 3145736 | tf_op jit(solution)/shard_map/ppermute | solution.py:17
  559.6 10.6 %collective-permute-done.15 = bf16[128,4096]{1,0:T(8,128)(2,1)S(1)} collective-permute-done((bf16[128,4096]{1,0:T(8,128)(2,1)S(1)}, bf16[128,4096]{1,0:T(8,128)(2,1)S(1)}, u32[]{:S(2)}, u32[]{:S(2)}) %collective-permute-start.15) | collective-permute-done | bytes 1048608 | tf_op jit(solution)/shard_map/ppermute | solution.py:17
  572.8 4.5 fusion.85
  577.3 19.8 %fusion.84 = bf16[1,512,2880]{1,2,0:T(8,128)(2,1)} fusion(bf16[4096,2880]{0,1:T(8,128)(2,1)} %all-gather.2.cloned.1.call-done, bf16[512,4096]{1,0:T(8,128)(2,1)} %select_dynamic-update-slice_fusion, pred[512]{0:T(512)(128)(4,1)S(1)} %iota_compare_fusion.3), kind=kOutput, calls=%fused_computation.116 | convolution fusion | flops 12083167232 | bytes 30736896 | tf_op jit(solution)/shard_map/dot_general | solution.py:178
  (410 shorter events, 236.5 us)
Async XLA Ops:
  7.2 10.3 %copy-start.4 = (s32[1,512,16]{1,2,0:T(8,128)S(1)}, s32[1,512,16]{1,2,0:T(8,128)}, u32[]{:S(2)}) copy-start(s32[1,512,16]{1,2,0:T(8,128)} %param.27) | copy-start | bytes 98308
  7.2 105.9 %copy-start.6 = (f32[64]{0:T(128)S(1)}, f32[64]{0:T(128)}, u32[]{:S(2)}) copy-start(f32[64]{0:T(128)} %param.30) | copy-start | bytes 772
  7.2 570.1 %all-gather.2.cloned.1.call-start = ((), (), s32[]{:S(2)}) async-start(), calls=%async_computation | async-start | bytes 24330240 | tf_op jit(solution)/shard_map/all_gather | solution.py:180
  10.7 100.2 %collective-permute-start.2 = (bf16[128,4096]{1,0:T(8,128)(2,1)S(1)}, bf16[128,4096]{1,0:T(8,128)(2,1)}, u32[]{:S(2)}, u32[]{:S(2)}) collective-permute-start(bf16[128,4096]{1,0:T(8,128)(2,1)S(1)} %get-tuple-element.501), channel_id=1, source_target_pairs={{0,8},{8,16},{16,24},{24,0},{1,9},{9,17},{17,25},{25,1},{2,10},{10... | collective-permute-start | bytes 3145736 | tf_op jit(solution)/shard_map/ppermute | solution.py:17
  11.8 100.9 %collective-permute-start.3 = (bf16[1024,512]{1,0:T(8,128)(2,1)}, bf16[1024,512]{1,0:T(8,128)(2,1)S(1)}, u32[]{:S(2)}, u32[]{:S(2)}) collective-permute-start(bf16[1024,512]{1,0:T(8,128)(2,1)} %bitcast.12), channel_id=1, source_target_pairs={{0,8},{8,16},{16,24},{24,0},{1,9},{9,17},{17,25},{25,1},{2,10},{10... | collective-permute-start | bytes 3145736 | tf_op jit(solution)/shard_map/ppermute | solution.py:17
  13.1 99.9 %collective-permute-start.5 = (bf16[1024,512]{1,0:T(8,128)(2,1)}, bf16[1024,512]{1,0:T(8,128)(2,1)}, u32[]{:S(2)}, u32[]{:S(2)}) collective-permute-start(bf16[1024,512]{1,0:T(8,128)(2,1)} %bitcast.14), channel_id=1, source_target_pairs={{0,8},{8,16},{16,24},{24,0},{1,9},{9,17},{17,25},{25,1},{2,10},{10... | collective-permute-start | bytes 3145736 | tf_op jit(solution)/shard_map/ppermute | solution.py:17
  15.3 82.1 %collective-permute-start.4 = (bf16[384,512]{1,0:T(8,128)(2,1)S(1)}, bf16[384,512]{1,0:T(8,128)(2,1)}, u32[]{:S(2)}, u32[]{:S(2)}) collective-permute-start(bf16[384,512]{1,0:T(8,128)(2,1)S(1)} %slice_bitcast_fusion.1), channel_id=1, source_target_pairs={{0,8},{8,16},{16,24},{24,0},{1,9},{9,17},{17,25},{25,1},{2,10},{10... | collective-permute-start | bytes 1179656 | tf_op jit(solution)/shard_map/ppermute | solution.py:17
  16.3 72.8 %collective-permute-start = (s32[2]{0:T(128)S(1)}, s32[2]{0:T(128)S(1)}, u32[]{:S(2)}, u32[]{:S(2)}) collective-permute-start(s32[2]{0:T(128)S(1)} %pad_add_fusion), channel_id=1, source_target_pairs={{0,8},{8,16},{16,24},{24,0},{1,9},{9,17},{17,25},{25,1},{2,10},{10... | collective-permute-start | bytes 32 | tf_op jit(solution)/shard_map/ppermute | solution.py:17
  89.2 3.4 collective-permute-start.1
  92.6 166.3 %collective-permute-start.12 = (bf16[512,512]{1,0:T(8,128)(2,1)}, bf16[512,512]{1,0:T(8,128)(2,1)S(1)}, u32[]{:S(2)}, u32[]{:S(2)}) collective-permute-start(bf16[512,512]{1,0:T(8,128)(2,1)} %bitcast.13), channel_id=1, source_target_pairs={{0,1},{1,2},{2,3},{3,4},{4,5},{5,6},{6,7},{7,0},{8,9},{9,10},{10,1... | collective-permute-start | bytes 1572872 | tf_op jit(solution)/shard_map/ppermute | solution.py:17
  97.4 13.4 %collective-permute-start.6 = (bf16[384,512]{1,0:T(8,128)(2,1)S(1)}, bf16[384,512]{1,0:T(8,128)(2,1)}, u32[]{:S(2)}, u32[]{:S(2)}) collective-permute-start(bf16[384,512]{1,0:T(8,128)(2,1)S(1)} %slice_bitcast_fusion), channel_id=1, source_target_pairs={{0,8},{8,16},{16,24},{24,0},{1,9},{9,17},{17,25},{25,1},{2,10},{10... | collective-permute-start | bytes 1179656 | tf_op jit(solution)/shard_map/ppermute | solution.py:17
  110.8 146.9 %collective-permute-start.9 = (s32[128,16]{0,1:T(8,128)S(1)}, s32[128,16]{0,1:T(8,128)S(1)}, u32[]{:S(2)}, u32[]{:S(2)}) collective-permute-start(s32[128,16]{0,1:T(8,128)S(1)} %get-tuple-element.502), channel_id=1, source_target_pairs={{0,1},{1,2},{2,3},{3,4},{4,5},{5,6},{6,7},{7,0},{8,9},{9,10},{10,1... | collective-permute-start | bytes 24584 | tf_op jit(solution)/shard_map/ppermute | solution.py:17
  110.9 298.8 %collective-permute-start.11 = (bf16[1024,512]{1,0:T(8,128)(2,1)}, bf16[1024,512]{1,0:T(8,128)(2,1)}, u32[]{:S(2)}, u32[]{:S(2)}) collective-permute-start(bf16[1024,512]{1,0:T(8,128)(2,1)} %bitcast.12), channel_id=1, source_target_pairs={{0,1},{1,2},{2,3},{3,4},{4,5},{5,6},{6,7},{7,0},{8,9},{9,10},{10,1... | collective-permute-start | bytes 3145736 | tf_op jit(solution)/shard_map/ppermute | solution.py:17
  112.8 296.9 %collective-permute-start.13 = (bf16[1024,512]{1,0:T(8,128)(2,1)}, bf16[1024,512]{1,0:T(8,128)(2,1)}, u32[]{:S(2)}, u32[]{:S(2)}) collective-permute-start(bf16[1024,512]{1,0:T(8,128)(2,1)} %bitcast.14), channel_id=1, source_target_pairs={{0,1},{1,2},{2,3},{3,4},{4,5},{5,6},{6,7},{7,0},{8,9},{9,10},{10,1... | collective-permute-start | bytes 3145736 | tf_op jit(solution)/shard_map/ppermute | solution.py:17
  113.0 144.7 %collective-permute-start.8 = (s32[2]{0:T(128)S(1)}, s32[2]{0:T(128)S(1)}, u32[]{:S(2)}, u32[]{:S(2)}) collective-permute-start(s32[2]{0:T(128)S(1)} %pad_add_fusion.1), channel_id=1, source_target_pairs={{0,1},{1,2},{2,3},{3,4},{4,5},{5,6},{6,7},{7,0},{8,9},{9,10},{10,1... | collective-permute-start | bytes 32 | tf_op jit(solution)/shard_map/ppermute | solution.py:17
  158.7 3.7 copy-start.1
  176.5 3.8 copy-start.1
  194.3 3.7 copy-start.1
  257.7 3.8 copy-start.7
  257.7 152.0 %collective-permute-start.10 = (bf16[128,4096]{1,0:T(8,128)(2,1)}, bf16[128,4096]{1,0:T(8,128)(2,1)}, u32[]{:S(2)}, u32[]{:S(2)}) collective-permute-start(bf16[128,4096]{1,0:T(8,128)(2,1)} %get-tuple-element.500), channel_id=1, source_target_pairs={{0,1},{1,2},{2,3},{3,4},{4,5},{5,6},{6,7},{7,0},{8,9},{9,10},{10,1... | collective-permute-start | bytes 3145736 | tf_op jit(solution)/shard_map/ppermute | solution.py:17
  257.7 3.8 copy-start.5
  257.7 152.0 %collective-permute-start.14 = (bf16[512,512]{1,0:T(8,128)(2,1)}, bf16[512,512]{1,0:T(8,128)(2,1)}, u32[]{:S(2)}, u32[]{:S(2)}) collective-permute-start(bf16[512,512]{1,0:T(8,128)(2,1)} %bitcast.15), channel_id=1, source_target_pairs={{0,1},{1,2},{2,3},{3,4},{4,5},{5,6},{6,7},{7,0},{8,9},{9,10},{10,1... | collective-permute-start | bytes 1572872 | tf_op jit(solution)/shard_map/ppermute | solution.py:17
  258.9 298.2 %collective-permute-start.7 = (bf16[128,4096]{1,0:T(8,128)(2,1)}, bf16[128,4096]{1,0:T(8,128)(2,1)}, u32[]{:S(2)}, u32[]{:S(2)}) collective-permute-start(bf16[128,4096]{1,0:T(8,128)(2,1)} %get-tuple-element.1062), channel_id=1, source_target_pairs={{0,24},{8,0},{16,8},{24,16},{1,25},{9,1},{17,9},{25,17},{2,26},{10... | collective-permute-start | bytes 3145736 | tf_op jit(solution)/shard_map/ppermute | solution.py:17
  409.8 160.3 %collective-permute-start.15 = (bf16[128,4096]{1,0:T(8,128)(2,1)S(1)}, bf16[128,4096]{1,0:T(8,128)(2,1)S(1)}, u32[]{:S(2)}, u32[]{:S(2)}) collective-permute-start(bf16[128,4096]{1,0:T(8,128)(2,1)S(1)} %get-tuple-element.1063), channel_id=1, source_target_pairs={{0,7},{1,0},{2,1},{3,2},{4,3},{5,4},{6,5},{7,6},{8,15},{9,8},{10,9... | collective-permute-start | bytes 3145736 | tf_op jit(solution)/shard_map/ppermute | solution.py:17
  (14 other events, 49.4 us)
Sparse Core Ops, SparseCore 0:
  97.6 164.9 all-gather.1
where the time goes:
time: 612 us; the launch traced here: 604 us
  starting transfers between devices  160 us (26%)
  matrix products  150 us (25%)
  waiting for transfers between devices  98.9 us (16%)
  other arithmetic  77.9 us (13%)
  local copies, waits for them, and re-layouts  67.4 us (11%)
  loops' own time  33.8 us (6%)
  between operations  16.1 us (3%)
    ppermute x16, starting transfers between devices, passed_along(): lax.ppermute(x, axis, [(i, (i + by) % length) for i in range(length)])  160 us
    ppermute x16, waiting for transfers between devices, passed_along(): lax.ppermute(x, axis, [(i, (i + by) % length) for i in range(length)])  98.9 us
    reduce_sum x16, other arithmetic, per_kv_head(): jnp.sum(weight_cache, axis=1)  52.6 us
    dot_general x16, matrix products, per_kv_head(): jnp.dot(q_part, key_cache.T, preferred_element_type=jnp.float32)  52 us
    dot_general x16, matrix products, per_kv_head(): jnp.dot(weight_cache.astype(jnp.bfloat16), value_cache, preferred_element...  34 us
    another operation x2, loops' own time, attend_rows(): per_head = lax.map(per_kv_head, jnp.arange(KVH, dtype=jnp.int32))  33.5 us
    dot_general x16, matrix products, per_kv_head(): jnp.dot(q_part, key_tree.T, preferred_element_type=jnp.float32)  22.7 us
    dot_general x16, matrix products, per_kv_head(): jnp.dot(weight_tree.astype(jnp.bfloat16), value_tree, preferred_element_t...  21.7 us
  transfers between devices with their start and end apart: 17, of which 4 were waited for; matrix products, arithmetic and copies ran while one was open for 45% of the time, Pallas kernels for 0%

commit v1 on v0

v1 whole, which is shorter than its diff:
```python
import functools

import jax
import jax.numpy as jnp
from jax import lax
from jax.experimental import pallas as pl
from jax.experimental.pallas import tpu as pltpu
from jax.sharding import PartitionSpec as P

KVH = 8
HD = 64
BLK = 128
MASKED = -1e30
AXES = ("gx", "gy")
VMEM_LIMIT = 60 * 1024 * 1024


def contract_last(a, b):
    return lax.dot_general(a, b, (((1,), (1,)), ((), ())), preferred_element_type=jnp.float32)


def attend_kernel(scal, q_ref, kc_ref, vc_ref, kt_ref, vt_ref, bias_ref, sink_ref, *rest):
    out_ref, kx, vx, qx = rest[-4:]
    head = pl.program_id(0)
    block = pl.program_id(1)
    cache_rows = kc_ref.shape[0]
    key_rows = kx.shape[0]
    groups = q_ref.shape[1] // HD

    @pl.when(block == 0)
    def _():
        src = lax.broadcasted_iota(jnp.int32, (BLK, BLK), 0)
        dst = lax.broadcasted_iota(jnp.int32, (BLK, BLK), 1)
        pick = jnp.where(src == (head % 2) * HD + dst % HD, 1.0, 0.0).astype(jnp.bfloat16)

        def both(x):
            return jnp.dot(x, pick, preferred_element_type=jnp.float32).astype(jnp.bfloat16)

        kx[0:cache_rows, 0:BLK] = both(kc_ref[...])
        kx[cache_rows:key_rows, 0:BLK] = both(kt_ref[...])
        vx[0:cache_rows, 0:BLK] = both(vc_ref[...])
        vx[cache_rows:key_rows, 0:BLK] = both(vt_ref[...])
        vx[:, BLK : 2 * BLK] = jnp.ones((key_rows, BLK), jnp.bfloat16)
        row = lax.broadcasted_iota(jnp.int32, (cache_rows, BLK), 0)
        kx[0:cache_rows, BLK : 2 * BLK] = jnp.where(row < scal[2], 0.0, MASKED).astype(jnp.bfloat16)
        own = jnp.where(src == dst, 1.0, 0.0).astype(jnp.bfloat16)
        for g in range(groups):
            qx[g * BLK : (g + 1) * BLK, BLK : 2 * BLK] = own

    live = block * BLK < scal[1]

    @pl.when(live)
    def _():
        kx[cache_rows:key_rows, BLK : 2 * BLK] = bias_ref[...]
        lane = lax.broadcasted_iota(jnp.int32, (BLK, BLK), 1)
        low = lane < HD
        node = lax.broadcasted_iota(jnp.int32, (BLK, BLK), 0) + block * BLK
        top = lax.broadcasted_iota(jnp.int32, (2 * BLK, 1), 0) < BLK
        zero = jnp.zeros((BLK, BLK), jnp.float32)
        for pair in range(groups // 2):
            cols = slice(pair * BLK, (pair + 1) * BLK)
            q2 = q_ref[:, cols].astype(jnp.float32) * (HD**-0.5)
            qx[(2 * pair) * BLK : (2 * pair + 1) * BLK, 0:BLK] = jnp.where(low, q2, zero).astype(
                jnp.bfloat16
            )
            qx[(2 * pair + 1) * BLK : (2 * pair + 2) * BLK, 0:BLK] = jnp.where(
                low, zero, q2
            ).astype(jnp.bfloat16)
        for pair in range(groups // 2):
            cols = slice(pair * BLK, (pair + 1) * BLK)
            rows = slice(2 * pair * BLK, (2 * pair + 2) * BLK)
            scores = contract_last(qx[rows, :], kx[...])
            sink = jnp.where(top, sink_ref[head * groups + 2 * pair], sink_ref[head * groups + 2 * pair + 1])
            peak = jnp.maximum(jnp.max(scores, axis=1, keepdims=True), sink)
            weights = jnp.exp(scores - peak).astype(jnp.bfloat16)
            sums = jnp.dot(weights, vx[...], preferred_element_type=jnp.float32)
            result = sums[:, 0:BLK] / (sums[:, BLK : 2 * BLK] + jnp.exp(sink - peak))
            joined = jnp.where(low, result[0:BLK], result[BLK : 2 * BLK])
            out_ref[:, cols] = jnp.where(node < scal[1], joined, zero).astype(out_ref.dtype)

    @pl.when(jnp.logical_not(live))
    def _():
        out_ref[...] = jnp.zeros_like(out_ref)


def attend(scal, q, k_cache, v_cache, k_tree, v_tree, bias, sinks, first, count, own, after):
    (q_arr, k_arr, v_arr, kt_arr, vt_arr), offsets, sizes = (
        (q, k_cache, v_cache, k_tree, v_tree),
        own["rows"],
        own["sizes"],
    )
    node_total = q_arr.shape[0]
    width = sinks.shape[0] // KVH * HD
    half = KVH // 2
    cache_rows, tree_rows = sizes
    whole = own["whole"]

    def col(s, h, per):
        base = s[0] * (half // per) if whole else 0
        return base + (first + h) // per

    def kv_spec(rows, at):
        return pl.BlockSpec((rows, BLK), lambda h, i, s: (at, col(s, h, 2)))

    grid_spec = pltpu.PrefetchScalarGridSpec(
        num_scalar_prefetch=1,
        grid=(count, node_total // BLK),
        in_specs=[
            pl.BlockSpec((BLK, width), lambda h, i, s: (i, col(s, h, 1))),
            kv_spec(cache_rows, offsets[0]),
            kv_spec(cache_rows, offsets[1]),
            kv_spec(tree_rows, offsets[2]),
            kv_spec(tree_rows, offsets[3]),
            pl.BlockSpec((tree_rows, BLK), lambda h, i, s: (0, i)),
            pl.BlockSpec(memory_space=pltpu.SMEM),
        ]
        + [pl.BlockSpec(memory_space=pl.ANY)] * len(after),
        out_specs=pl.BlockSpec((BLK, width), lambda h, i, s: (i, h)),
        scratch_shapes=[
            pltpu.VMEM((cache_rows + tree_rows, 2 * BLK), jnp.bfloat16),
            pltpu.VMEM((cache_rows + tree_rows, 2 * BLK), jnp.bfloat16),
            pltpu.VMEM((width // HD * BLK, 2 * BLK), jnp.bfloat16),
        ],
    )
    groups = width // HD
    keys = cache_rows + tree_rows
    rows = count * groups * node_total // 2
    half_sinks = lax.dynamic_slice(
        sinks, (scal[0] * (half * groups) + first * groups,), (count * groups,)
    )
    return pl.pallas_call(
        attend_kernel,
        grid_spec=grid_spec,
        out_shape=jax.ShapeDtypeStruct((node_total, count * width), jnp.bfloat16),
        compiler_params=pltpu.CompilerParams(vmem_limit_bytes=VMEM_LIMIT),
        cost_estimate=pl.CostEstimate(
            flops=rows * keys * 2 * 512,
            bytes_accessed=4 * keys * BLK * 2,
            transcendentals=rows * keys,
        ),
        name="attend",
    )(scal, q_arr, k_arr, v_arr, kt_arr, vt_arr, bias, half_sinks, *after)


def tree_bias(words_t, key_total):
    spread = jnp.repeat(words_t, 32, axis=0)
    shift = (jnp.arange(key_total, dtype=jnp.int32) % 32)[:, None]
    flag = jnp.bitwise_and(lax.shift_right_logical(spread, jnp.broadcast_to(shift, spread.shape)), 1)
    return jnp.where(flag > 0, 0.0, MASKED).astype(jnp.bfloat16)


def project_kernel(plan, last, has_acc, info, busy_ref, light_ref, *refs):
    refs = list(refs)
    acc_in = refs.pop(0) if has_acc else None
    blocks = refs[: len(plan)]
    refs = refs[len(plan) :]
    if last:
        own_ref, other_ref, acc = refs
    else:
        (acc,) = refs
    busy_rows = busy_ref.shape[0]
    light_rows = light_ref.shape[0]
    if has_acc:
        acc[...] = acc_in[...]
    started = has_acc
    for at, (slot, low, high) in enumerate(plan):
        block = blocks[at][...]
        depth = block.shape[1]
        cols = pl.ds(pl.multiple_of(info[slot] * depth, depth), depth)
        for x_ref, base, rows in ((busy_ref, 0, busy_rows), (light_ref, busy_rows, light_rows)):
            part = contract_last(x_ref[:, cols], block)
            where = (slice(base, base + rows), slice(low, high))
            if started:
                acc[where] += part
            else:
                acc[where] = part
        started = True
    if last:
        done = acc[...].astype(jnp.bfloat16)
        busy, light = done[:busy_rows], done[busy_rows:]
        rest = jnp.zeros((busy_rows - light_rows, done.shape[1]), jnp.bfloat16)

        @pl.when(info[len(info_slots())] > 0)
        def _():
            own_ref[...] = busy
            other_ref[0:light_rows, :] = light
            other_ref[light_rows:, :] = rest

        @pl.when(info[len(info_slots())] <= 0)
        def _():
            other_ref[...] = busy
            own_ref[0:light_rows, :] = light
            own_ref[light_rows:, :] = rest


def info_slots():
    return tuple(range(16))


def project(info, busy, light, acc, blocks, plan, columns, last):
    rows = busy.shape[0] + light.shape[0]
    acc_shape = jax.ShapeDtypeStruct((rows, columns), jnp.float32)
    half = jax.ShapeDtypeStruct((busy.shape[0], columns), jnp.bfloat16)
    vmem = pl.BlockSpec(memory_space=pltpu.VMEM)
    operands = [info, busy, light] + ([] if acc is None else [acc]) + list(blocks)
    flops = sum(2 * rows * b.size for b in blocks)
    return pl.pallas_call(
        functools.partial(project_kernel, plan, last, acc is not None),
        out_shape=(half, half) if last else acc_shape,
        in_specs=[pl.BlockSpec(memory_space=pltpu.SMEM)] + [vmem] * (len(operands) - 1),
        out_specs=(vmem, vmem) if last else vmem,
        scratch_shapes=[pltpu.VMEM((rows, columns), jnp.float32)] if last else [],
        compiler_params=pltpu.CompilerParams(vmem_limit_bytes=VMEM_LIMIT),
        cost_estimate=pl.CostEstimate(flops=flops, bytes_accessed=rows * columns * 8, transcendentals=0),
        name="project",
    )(*operands)


def on_device(plane, line, args):
    (
        q_nodes, k_cache, v_cache, k_tree, v_tree, anc_bits, node_count, cache_len, sinks, o_weight,
    ) = args
    gx = lax.axis_index("gx")
    gy = lax.axis_index("gy")
    core = gy % 2
    z = gy // 2
    places = [(a, b, c) for a in range(plane) for b in range(line) for c in range(2)]

    def number(a, b, c):
        return (a * line + b) * 2 + c

    def moved(x, to):
        pairs = [(number(*p), number(*to(*p))) for p in places]
        return lax.ppermute(x, AXES, pairs)

    def swapped(x):
        return moved(x, lambda a, b, c: (a, b, 1 - c))

    q, kc, vc, kt, vt = q_nodes[0], k_cache[0], v_cache[0], k_tree[0], v_tree[0]
    node_total = q.shape[0]
    cache_rows, tree_rows = kc.shape[0], kt.shape[0]
    columns = o_weight.shape[1] // 2
    half_q, half_kv = q.shape[1] // 2, kc.shape[1] // 2
    far = 1 - core

    w_t = o_weight.T
    w_mine = lax.dynamic_slice_in_dim(w_t, core * columns, columns, 0)
    w_theirs = swapped(lax.dynamic_slice_in_dim(w_t, far * columns, columns, 0))
    own_block = jnp.where(
        core == 0,
        jnp.concatenate([w_mine, w_theirs], axis=1),
        jnp.concatenate([w_theirs, w_mine], axis=1),
    )

    words_t = anc_bits[0].T
    counts = jnp.concatenate([node_count, cache_len])
    note = jnp.concatenate([words_t, jnp.broadcast_to(counts[:, None], (2, node_total))], axis=0)
    q_away = lax.dynamic_slice_in_dim(q, far * half_q, half_q, 1)
    kv_away = jnp.concatenate(
        [lax.dynamic_slice_in_dim(a, far * half_kv, half_kv, 1) for a in (kc, vc, kt, vt)], axis=0
    )
    q_got, kv_got, note_got = swapped(q_away), swapped(kv_away), swapped(note)

    bias = tree_bias(words_t, tree_rows)
    scal = jnp.stack([core, node_count[0], cache_len[0]]).astype(jnp.int32)
    own = dict(rows=(0, 0, 0, 0), sizes=(cache_rows, tree_rows), whole=True)
    ratio = cache_rows // tree_rows
    got = dict(rows=(0, 1, 2 * ratio, 2 * ratio + 1), sizes=(cache_rows, tree_rows), whole=False)
    word_total = words_t.shape[0]
    bias_got = tree_bias(note_got[:word_total], tree_rows)
    scal_got = jnp.stack([core, note_got[word_total, 0], note_got[word_total + 1, 0]]).astype(jnp.int32)

    def attend_own(first, after):
        return attend(scal, q, kc, vc, kt, vt, bias, sinks, first, KVH // 4, own, after)

    def attend_got(first, after):
        return attend(
            scal_got, q_got, kv_got, kv_got, kv_got, kv_got, bias_got, sinks, first, KVH // 4, got, after
        )

    chips = plane * line
    direct = plane == 4 and line == 4

    if direct:
        def along_x(x):
            return moved(x, lambda a, b, c: (a ^ 1, b, c))

        def along_y(x):
            return moved(x, lambda a, b, c: (a ^ 2, b, c))

        def along_z(x, by):
            return moved(x, lambda a, b, c: (a, (b + by) % line, c))

        cut = columns // (2 * BLK) * BLK + BLK
        b0 = own_block
        x0, y0 = along_x(b0), along_y(b0)
        z1, z3, z2 = along_z(b0, 1), along_z(b0, 3), along_z(b0, 2)

        def diagonal(xk, yk):
            return along_x(yk[:cut]), along_y(xk[cut:])

        mine01 = attend_own(0, ())
        d0 = diagonal(x0, y0)
        x1, y1 = along_x(z1), along_y(z1)
        theirs01 = attend_got(0, (x0, y0, z1))
        d1 = diagonal(x1, y1)
        x3, y3 = along_x(z3), along_y(z3)
        mine23 = attend_own(KVH // 4, (x1, y1, z3, *d0))
        theirs23 = attend_got(KVH // 4, (x1, y1, z3, *d0))
        d3 = diagonal(x3, y3)
        x2, y2 = along_x(z2), along_y(z2)
        d2 = diagonal(x2, y2)
    else:
        mine01 = attend_own(0, ())
        theirs01 = attend_got(0, ())
        mine23 = attend_own(KVH // 4, ())
        theirs23 = attend_got(KVH // 4, ())

    mine = jnp.concatenate([mine01, mine23], axis=1)
    theirs = jnp.concatenate([theirs01, theirs23], axis=1)
    mine_back = jnp.concatenate([swapped(theirs01), swapped(theirs23)], axis=1)
    theirs_own = jnp.concatenate([swapped(mine01), swapped(mine23)], axis=1)

    def in_order(here, there):
        return jnp.where(
            core == 0,
            jnp.concatenate([here, there], axis=1),
            jnp.concatenate([there, here], axis=1),
        )

    attended = in_order(mine, mine_back)
    other = in_order(theirs, theirs_own)
    is_busy = (gx + gy) % 2 == 0
    busy = jnp.where(is_busy, attended, other)
    light = jnp.where(is_busy, other[:BLK], attended[:BLK])

    if direct:
        places_of = {}
        slots = []
        for dz in (0, 1, 3, 2):
            for flip in (0, 1, 2, 3):
                places_of[(dz, flip)] = len(slots)
                slots.append((gx ^ flip) * line + (z - dz) % line)
        info = jnp.stack(slots + [is_busy.astype(jnp.int32)]).astype(jnp.int32)

        def whole(dz, flip):
            return (places_of[(dz, flip)], 0, columns)

        def halves(dz):
            at = places_of[(dz, 3)]
            return [(at, 0, cut), (at, cut, columns)]

        early = [b0, x0, y0, z1, x1, y1, *d0]
        early_plan = [whole(0, 0), whole(0, 1), whole(0, 2), whole(1, 0), whole(1, 1), whole(1, 2)]
        early_plan += halves(0)
        acc = project(info, busy, light, None, early, early_plan, columns, False)
        late = [z3, x3, y3, *d1, z2]
        late_plan = [whole(3, 0), whole(3, 1), whole(3, 2), *halves(1), whole(2, 0)]
        acc = project(info, busy, light, acc, late, late_plan, columns, False)
        end = [x2, y2, *d3, *d2]
        end_plan = [whole(2, 1), whole(2, 2), *halves(3), *halves(2)]
        own_half, other_half = project(info, busy, light, acc, end, end_plan, columns, True)
    else:
        w_all = lax.all_gather(o_weight, AXES, axis=0, tiled=True)
        w_half = lax.dynamic_slice_in_dim(w_all, core * columns, columns, 1)

        def dot(x):
            return jnp.dot(x, w_half, preferred_element_type=jnp.float32).astype(jnp.bfloat16)

        own_half, other_half = dot(attended), dot(other)

    projected = in_order(own_half, swapped(other_half))
    return attended[None], projected[None]


def solution(mesh):
    plane, line = mesh.shape["gx"], mesh.shape["gy"] // 2
    rows = P(AXES, None, None)
    placed = (rows, rows, rows, rows, rows, rows, P(AXES), P(AXES), P(), P(AXES, None))

    def run(*args):
        return on_device(plane, line, args)

    return jax.shard_map(run, mesh=mesh, in_specs=placed, out_specs=(rows, rows), check_vma=False)
```

time: 612 us -> 244 us (0.40); the launches traced: 604 us -> 242 us
  matrix products: 150 us -> 0 us
  starting transfers between devices: 160 us -> 48.3 us
  Pallas kernels: 0 us -> 105 us
  waiting for transfers between devices: 98.9 us -> 31.5 us
  other arithmetic: 77.9 us -> 26 us
  local copies, waits for them, and re-layouts: 67.4 us -> 29.7 us
  loops' own time: 33.8 us -> 0 us
  between operations: 16.1 us -> 2.18 us
    dot_general x65 -> x0, matrix products: 150 us -> none  [the longest x16 52 us: per_kv_head(): jnp.dot(q_part, key_cache.T, preferred_element_type=jnp.float32)]
    ppermute x16 -> x28, starting transfers between devices: 160 us -> 48.3 us  [moved(): return lax.ppermute(x, AXES, pairs)]
    pallas_call x0 -> x7, Pallas kernels: none -> 105 us  [the longest x4 75.2 us: attend(): pl.pallas_call(attend_kernel, grid_spec=grid_spec, out_shape=jax.ShapeDty...]
    ppermute x16 -> x28, waiting for transfers between devices: 98.9 us -> 31.5 us  [moved(): return lax.ppermute(x, AXES, pairs)]
    reduce_sum x32 -> x0, other arithmetic: 57.2 us -> none  [the longest x16 52.6 us: per_kv_head(): jnp.sum(weight_cache, axis=1)]
    another operation x5 -> x0, loops' own time: 33.8 us -> none  [the longest x2 33.5 us: attend_rows(): per_head = lax.map(per_kv_head, jnp.arange(KVH, dtype=jnp.int32))]
    select_n x0 -> x6, other arithmetic: none -> 20.1 us  [the longest x2 10.3 us: in_order(): jnp.where(core == 0, jnp.concatenate([here, there], axis=1), jnp.concaten...]
    dynamic_slice x52 -> x5, local copies, waits for them, and re-layouts: 23.3 us -> 4.81 us  [the longest x1 1.88 us: on_device(): q_away = lax.dynamic_slice_in_dim(q, far * half_q, half_q, 1)]
  transfers between devices with their start and end apart: 17 -> 28, of which waited for: 4 -> 4; matrix products, arithmetic and copies ran while one was open for 45% -> 16% of each run, Pallas kernels for 0% -> 39%
where the time goes in v1:
time: 244 us; the launch traced here: 242 us
  Pallas kernels  105 us (43%)
  starting transfers between devices  48.3 us (20%)
  waiting for transfers between devices  31.5 us (13%)
  local copies, waits for them, and re-layouts  29.7 us (12%)
  other arithmetic  26 us (11%)
    pallas_call x4, Pallas kernels, attend(): pl.pallas_call(attend_kernel, grid_spec=grid_spec, out_shape=jax.ShapeDty...  75.2 us
    ppermute x28, starting transfers between devices, moved(): return lax.ppermute(x, AXES, pairs)  48.3 us
    ppermute x28, waiting for transfers between devices, moved(): return lax.ppermute(x, AXES, pairs)  31.5 us
    pallas_call x3, Pallas kernels, project(): pl.pallas_call(functools.partial(project_kernel, plan, last, acc is not N...  29.4 us
    slice x8, local copies, waits for them, and re-layouts, diagonal(): return (along_x(yk[:cut]), along_y(xk[cut:]))  12.6 us
    select_n x2, other arithmetic, in_order(): jnp.where(core == 0, jnp.concatenate([here, there], axis=1), jnp.concaten...  10.3 us
    select_n x1, other arithmetic, on_device(): busy = jnp.where(is_busy, attended, other)  8.43 us
    unnamed x29, local copies, waits for them, and re-layouts  5 us
  transfers between devices with their start and end apart: 28, of which 4 were waited for; matrix products, arithmetic and copies ran while one was open for 16% of the time, Pallas kernels for 39%

profile of v1, /device:TPU:9, one launch (start us, length us, event | category | flops | bytes accessed | tf_op | source)
XLA Modules:
  0.0 242.4 jit_solution(9838206207228953399)
XLA Ops:
  6.9 1.9 dynamic-slice_bitcast_fusion
  12.8 9.5 %collective-permute-done.7.rest_0_.refs_1_ = bf16[1440,256]{1,0:T(8,128)(2,1)} collective-permute-done((bf16[1440,256]{1,0:T(8,128)(2,1)S(1)}, bf16[1440,256]{1,0:T(8,128)(2,1)}, u32[]{:S(2)}, u32[]{:S(2)}) %collective-permute-start.7) | collective-permute-done | bytes 737312 | tf_op jit(solution)/shard_map/ppermute | solution.py:234
  32.8 12.6 %collective-permute-done.4.rest_2_.refs_1_ = bf16[1440,256]{1,0:T(8,128)(2,1)} collective-permute-done((bf16[1440,256]{1,0:T(8,128)(2,1)S(1)}, bf16[1440,256]{1,0:T(8,128)(2,1)}, u32[]{:S(2)}, u32[]{:S(2)}) %collective-permute-start.4) | collective-permute-done | bytes 737312 | tf_op jit(solution)/shard_map/ppermute | solution.py:234
  45.9 12.7 %attend.4 = bf16[512,1024]{1,0:T(8,128)(2,1)} custom-call(s32[3]{0:T(128)} %pad_add_fusion.1.scal, bf16[512,4096]{1,0:T(8,128)(2,1)} %bitcast.69, bf16[1024,512]{1,0:T(8,128)(2,1)} %bitcast.73, bf16[1024,512]{1,0:T(8,128)(2,1)} %bitcast.71, bf16[512,512]{1,0:T(8,128)(2,1)} %bitcast.79, bf16[512,512]{1,0:T(8,128)(2,1)} %bitcast.77, ...), custom_call_target="tpu_custom_call" | custom-call | flops 6442450944 | bytes 1572864 | tf_op jit(solution)/shard_map/attend/pallas_call | solution.py:131
  60.6 1.9 pad_add_fusion.3.scal
  63.3 15.3 %collective-permute-start.14 = (bf16[512,1024]{1,0:T(8,128)(2,1)}, bf16[512,1024]{1,0:T(8,128)(2,1)}, u32[]{:S(2)}, u32[]{:S(2)}) collective-permute-start(bf16[512,1024]{1,0:T(8,128)(2,1)} %attend.4), channel_id=1, source_target_pairs={{0,1},{1,0},{2,3},{3,2},{4,5},{5,4},{6,7},{7,6},{8,9},{9,8},{10,11... | collective-permute-start | bytes 3145736 | tf_op jit(solution)/shard_map/ppermute | solution.py:234
  78.6 12.7 %attend.5 = bf16[512,1024]{1,0:T(8,128)(2,1)} custom-call(s32[3]{0:T(128)} %pad_add_fusion.1.scal, bf16[512,4096]{1,0:T(8,128)(2,1)} %bitcast.70, bf16[1024,512]{1,0:T(8,128)(2,1)} %bitcast.74, bf16[1024,512]{1,0:T(8,128)(2,1)} %bitcast.72, bf16[512,512]{1,0:T(8,128)(2,1)} %bitcast.80, bf16[512,512]{1,0:T(8,128)(2,1)} %bitcast.78, ...), custom_call_target="tpu_custom_call" | custom-call | flops 6442450944 | bytes 1572864 | tf_op jit(solution)/shard_map/attend/pallas_call | solution.py:131
  92.9 13.1 %collective-permute-start.15 = (bf16[512,1024]{1,0:T(8,128)(2,1)}, bf16[512,1024]{1,0:T(8,128)(2,1)}, u32[]{:S(2)}, u32[]{:S(2)}) collective-permute-start(bf16[512,1024]{1,0:T(8,128)(2,1)} %attend.5), channel_id=1, source_target_pairs={{0,1},{1,0},{2,3},{3,2},{4,5},{5,4},{6,7},{7,6},{8,9},{9,8},{10,11... | collective-permute-start | bytes 3145736 | tf_op jit(solution)/shard_map/ppermute | solution.py:234
  105.9 24.8 %attend.6 = bf16[512,1024]{1,0:T(8,128)(2,1)} custom-call(s32[3]{0:T(128)} %pad_add_fusion.3.scal, bf16[512,2048]{1,0:T(8,128)(2,1)} %collective-permute-done.10.q_ref, bf16[3072,256]{1,0:T(8,128)(2,1)} %collective-permute-done.11.kc_ref.vc_ref.kt_ref.vt_ref, bf16[3072,256]{1,0:T(8,128)(2,1)} %collective-permute-done.11.kc_ref.vc_ref.kt_ref.vt_ref, ...), custom_call_target="tpu_custom_call" | custom-call | flops 6442450944 | bytes 1572864 | tf_op jit(solution)/shard_map/attend/pallas_call | solution.py:131
  130.8 25.0 %attend.7 = bf16[512,1024]{1,0:T(8,128)(2,1)} custom-call(s32[3]{0:T(128)} %pad_add_fusion.3.scal, bf16[512,2048]{1,0:T(8,128)(2,1)} %collective-permute-done.10.q_ref, bf16[3072,256]{1,0:T(8,128)(2,1)} %collective-permute-done.11.kc_ref.vc_ref.kt_ref.vt_ref, bf16[3072,256]{1,0:T(8,128)(2,1)} %collective-permute-done.11.kc_ref.vc_ref.kt_ref.vt_ref, ...), custom_call_target="tpu_custom_call" | custom-call | flops 6442450944 | bytes 1572864 | tf_op jit(solution)/shard_map/attend/pallas_call | solution.py:131
  158.0 1.9 slice.59
  160.9 1.8 slice.61
  162.6 1.8 slice.63
  166.1 8.5 %collective-permute-done.21.refs_1_ = bf16[1440,256]{1,0:T(8,128)(2,1)} collective-permute-done((bf16[1440,256]{1,0:T(8,128)(2,1)}, bf16[1440,256]{1,0:T(8,128)(2,1)}, u32[]{:S(2)}, u32[]{:S(2)}) %collective-permute-start.21) | collective-permute-done | bytes 737312 | tf_op jit(solution)/shard_map/ppermute | solution.py:234
  179.9 8.4 %broadcast_select_fusion = (bf16[512,4096]{1,0:T(8,128)(2,1)}, bf16[512,4096]{1,0:T(8,128)(2,1)S(1)}, bf16[512,4096]{1,0:T(8,128)(2,1)S(1)}) fusion(pred[]{:T(512)S(6)} %eq.32, bf16[512,1024]{1,0:T(8,128)(2,1)S(1)} %copy-done.4, bf16[512,1024]{1,0:T(8,128)(2,1)S(1)} %copy-done.3, bf16[512,1024]{1,0:T(8,128)(2,1)} %collective-permute-done.15, ...), kind=kLoop, calls=%fused_computation.3 | loop fusion | flops 73400320 | bytes 20971522 | tf_op jit(solution)/shard_map/jit(_where)/select_n | solution.py:334
  190.2 10.4 %project.3.refs_0_ = f32[640,1440]{1,0:T(8,128)} custom-call(s32[17]{0:T(128)} %stack.88.info, bf16[512,4096]{1,0:T(8,128)(2,1)} %get-tuple-element.10.busy_ref, bf16[128,4096]{1,0:T(8,128)(2,1)} %slice_select_fusion.light_ref, bf16[1440,256]{1,0:T(8,128)(2,1)} %copy-done.2, bf16[1440,256]{1,0:T(8,128)(2,1)} %collective-permute-done.7.rest_0_.refs_1_, ...), custom_call_target="tpu_custom_call" | custom-call | flops 3303014400 | bytes 7372800 | tf_op jit(solution)/shard_map/project/pallas_call | solution.py:207
  200.7 9.8 %project.4.refs_0_ = f32[640,1440]{1,0:T(8,128)} custom-call(s32[17]{0:T(128)} %stack.88.info, bf16[512,4096]{1,0:T(8,128)(2,1)} %get-tuple-element.10.busy_ref, bf16[128,4096]{1,0:T(8,128)(2,1)} %slice_select_fusion.light_ref, f32[640,1440]{1,0:T(8,128)} %project.3.refs_0_, bf16[1440,256]{1,0:T(8,128)(2,1)} %collective-permute-done.4.rest_2_.refs_1_, ...), custom_call_target="tpu_custom_call" | custom-call | flops 2359296000 | bytes 7372800 | tf_op jit(solution)/shard_map/project/pallas_call | solution.py:207
  212.0 9.2 %project.5 = (bf16[512,1440]{1,0:T(8,128)(2,1)}, bf16[512,1440]{1,0:T(8,128)(2,1)}) custom-call(s32[17]{0:T(128)} %stack.88.info, bf16[512,4096]{1,0:T(8,128)(2,1)} %get-tuple-element.10.busy_ref, bf16[128,4096]{1,0:T(8,128)(2,1)} %slice_select_fusion.light_ref, f32[640,1440]{1,0:T(8,128)} %project.4.refs_0_, ...), custom_call_target="tpu_custom_call" | custom-call | flops 1887436800 | bytes 7372800 | tf_op jit(solution)/shard_map/project/pallas_call | solution.py:207
  221.2 2.6 %copy.13 = bf16[512,1440]{0,1:T(8,128)(2,1)} copy(bf16[512,1440]{1,0:T(8,128)(2,1)} %get-tuple-element.5) | data formatting | bytes 2949120 | tf_op jit(solution)/shard_map/project/pallas_call | solution.py:207
  223.8 3.0 %collective-permute-start.27 = (bf16[512,1440]{0,1:T(8,128)(2,1)}, bf16[512,1440]{0,1:T(8,128)(2,1)}, u32[]{:S(2)}, u32[]{:S(2)}) collective-permute-start(bf16[512,1440]{0,1:T(8,128)(2,1)} %copy.13), channel_id=1, source_target_pairs={{0,1},{1,0},{2,3},{3,2},{4,5},{5,4},{6,7},{7,6},{8,9},{9,8},{10,11... | collective-permute-start | bytes 4423688 | tf_op jit(solution)/shard_map/ppermute | solution.py:234
  226.8 4.5 %maximum_select_fusion = bf16[1,512,4096]{2,1,0:T(8,128)(2,1)} fusion(bf16[1,512,1024]{2,1,0:T(8,128)(2,1)} %bitcast.23, bf16[1,512,1024]{2,1,0:T(8,128)(2,1)S(1)} %bitcast.67, bf16[1,512,1024]{2,1,0:T(8,128)(2,1)S(1)} %bitcast.66, bf16[1,512,1024]{2,1,0:T(8,128)(2,1)S(1)} %bitcast.65, pred[]{:T(512)S(6)} %eq.31), kind=kLoop, calls=%fused_computation | loop fusion | flops 35651584 | bytes 8388609 | tf_op jit(solution)/shard_map/jit(_where)/select_n | solution.py:325
  231.2 2.6 %copy.14 = bf16[512,1440]{1,0:T(8,128)(2,1)} copy(bf16[512,1440]{0,1:T(8,128)(2,1)} %collective-permute-done.27) | data formatting | bytes 2949120 | tf_op jit(solution)/shard_map/ppermute | solution.py:234
  233.8 5.9 %maximum_select_fusion.3 = bf16[1,512,2880]{2,1,0:T(8,128)(2,1)S(1)} fusion(bf16[1,512,1440]{2,1,0:T(8,128)(2,1)} %bitcast.64, bf16[1,512,1440]{2,1,0:T(8,128)(2,1)} %bitcast.68, pred[]{:T(512)S(6)} %eq.31), kind=kLoop, calls=%fused_computation.4 | loop fusion | flops 13271040 | bytes 5898241 | tf_op jit(solution)/shard_map/jit(_where)/select_n | solution.py:325
  239.7 2.7 %copy.15 = bf16[1,512,2880]{1,2,0:T(8,128)(2,1)} copy(bf16[1,512,2880]{2,1,0:T(8,128)(2,1)S(1)} %maximum_select_fusion.3) | data formatting | bytes 5898240
  (99 shorter events, 37.7 us)
Async XLA Ops:
  4.3 18.0 %collective-permute-start.7 = (bf16[1440,256]{1,0:T(8,128)(2,1)S(1)}, bf16[1440,256]{1,0:T(8,128)(2,1)}, u32[]{:S(2)}, u32[]{:S(2)}) collective-permute-start(bf16[1440,256]{1,0:T(8,128)(2,1)S(1)} %maximum_select_fusion.4.refs_0_), channel_id=1, source_target_pairs={{0,8},{1,9},{2,10},{3,11},{4,12},{5,13},{6,14},{7,15},{8,0},{9,1},... | collective-permute-start | bytes 2211848 | tf_op jit(solution)/shard_map/ppermute | solution.py:234
  6.4 18.7 %collective-permute-start.9 = (s32[18,512]{1,0:T(8,128)S(1)}, s32[18,512]{1,0:T(8,128)S(1)}, u32[]{:S(2)}, u32[]{:S(2)}) collective-permute-start(s32[18,512]{1,0:T(8,128)S(1)} %pad_add_fusion), channel_id=1, source_target_pairs={{0,1},{1,0},{2,3},{3,2},{4,5},{5,4},{6,7},{7,6},{8,9},{9,8},{10,11... | collective-permute-start | bytes 110600 | tf_op jit(solution)/shard_map/ppermute | solution.py:234
  8.8 19.4 %collective-permute-start.5 = (bf16[1440,256]{1,0:T(8,128)(2,1)S(1)}, bf16[1440,256]{1,0:T(8,128)(2,1)}, u32[]{:S(2)}, u32[]{:S(2)}) collective-permute-start(bf16[1440,256]{1,0:T(8,128)(2,1)S(1)} %maximum_select_fusion.4.refs_0_), channel_id=1, source_target_pairs={{0,16},{1,17},{2,18},{3,19},{4,20},{5,21},{6,22},{7,23},{8,24},{9,... | collective-permute-start | bytes 2211848 | tf_op jit(solution)/shard_map/ppermute | solution.py:234
  10.2 21.3 %collective-permute-start.1 = (bf16[1440,256]{1,0:T(8,128)(2,1)S(1)}, bf16[1440,256]{1,0:T(8,128)(2,1)}, u32[]{:S(2)}, u32[]{:S(2)}) collective-permute-start(bf16[1440,256]{1,0:T(8,128)(2,1)S(1)} %maximum_select_fusion.4.refs_0_), channel_id=1, source_target_pairs={{0,2},{1,3},{2,4},{3,5},{4,6},{5,7},{6,0},{7,1},{8,10},{9,11},{10,... | collective-permute-start | bytes 2211848 | tf_op jit(solution)/shard_map/ppermute | solution.py:234
  11.6 33.9 %collective-permute-start.4 = (bf16[1440,256]{1,0:T(8,128)(2,1)S(1)}, bf16[1440,256]{1,0:T(8,128)(2,1)}, u32[]{:S(2)}, u32[]{:S(2)}) collective-permute-start(bf16[1440,256]{1,0:T(8,128)(2,1)S(1)} %maximum_select_fusion.4.refs_0_), channel_id=1, source_target_pairs={{0,6},{1,7},{2,0},{3,1},{4,2},{5,3},{6,4},{7,5},{8,14},{9,15},{10,... | collective-permute-start | bytes 2211848 | tf_op jit(solution)/shard_map/ppermute | solution.py:234
  22.3 70.6 %collective-permute-start.10 = (bf16[512,2048]{1,0:T(8,128)(2,1)S(1)}, bf16[512,2048]{1,0:T(8,128)(2,1)}, u32[]{:S(2)}, u32[]{:S(2)}) collective-permute-start(bf16[512,2048]{1,0:T(8,128)(2,1)S(1)} %dynamic-slice_bitcast_fusion), channel_id=1, source_target_pairs={{0,1},{1,0},{2,3},{3,2},{4,5},{5,4},{6,7},{7,6},{8,9},{9,8},{10,11... | collective-permute-start | bytes 6291464 | tf_op jit(solution)/shard_map/ppermute | solution.py:234
  25.1 20.6 %collective-permute-start.8 = (bf16[672,256]{1,0:T(8,128)(2,1)}, bf16[672,256]{1,0:T(8,128)(2,1)}, u32[]{:S(2)}, u32[]{:S(2)}) collective-permute-start(bf16[672,256]{1,0:T(8,128)(2,1)} %slice.53), channel_id=1, source_target_pairs={{0,16},{1,17},{2,18},{3,19},{4,20},{5,21},{6,22},{7,23},{8,24},{9,... | collective-permute-start | bytes 1032200 | tf_op jit(solution)/shard_map/ppermute | solution.py:234
  28.2 63.2 %collective-permute-start.11 = (bf16[3072,256]{1,0:T(8,128)(2,1)}, bf16[3072,256]{1,0:T(8,128)(2,1)}, u32[]{:S(2)}, u32[]{:S(2)}) collective-permute-start(bf16[3072,256]{1,0:T(8,128)(2,1)} %pad_maximum_fusion), channel_id=1, source_target_pairs={{0,1},{1,0},{2,3},{3,2},{4,5},{5,4},{6,7},{7,6},{8,9},{9,8},{10,11... | collective-permute-start | bytes 4718600 | tf_op jit(solution)/shard_map/ppermute | solution.py:234
  31.5 27.1 %collective-permute-start.6 = (bf16[768,256]{1,0:T(8,128)(2,1)S(1)}, bf16[768,256]{1,0:T(8,128)(2,1)S(1)}, u32[]{:S(2)}, u32[]{:S(2)}) collective-permute-start(bf16[768,256]{1,0:T(8,128)(2,1)S(1)} %slice.52), channel_id=1, source_target_pairs={{0,8},{1,9},{2,10},{3,11},{4,12},{5,13},{6,14},{7,15},{8,0},{9,1},... | collective-permute-start | bytes 1179656 | tf_op jit(solution)/shard_map/ppermute | solution.py:234
  45.7 32.9 %collective-permute-start.3 = (bf16[1440,256]{1,0:T(8,128)(2,1)}, bf16[1440,256]{1,0:T(8,128)(2,1)}, u32[]{:S(2)}, u32[]{:S(2)}) collective-permute-start(bf16[1440,256]{1,0:T(8,128)(2,1)} %collective-permute-done.1.rest_2_.refs_3_), channel_id=1, source_target_pairs={{0,16},{1,17},{2,18},{3,19},{4,20},{5,21},{6,22},{7,23},{8,24},{9,... | collective-permute-start | bytes 2211848 | tf_op jit(solution)/shard_map/ppermute | solution.py:234
  58.6 32.7 %collective-permute-start.20 = (bf16[1440,256]{1,0:T(8,128)(2,1)S(1)}, bf16[1440,256]{1,0:T(8,128)(2,1)}, u32[]{:S(2)}, u32[]{:S(2)}) collective-permute-start(bf16[1440,256]{1,0:T(8,128)(2,1)S(1)} %maximum_select_fusion.4.refs_0_), channel_id=1, source_target_pairs={{0,4},{1,5},{2,6},{3,7},{4,0},{5,1},{6,2},{7,3},{8,12},{9,13},{10,... | collective-permute-start | bytes 2211848 | tf_op jit(solution)/shard_map/ppermute | solution.py:234
  63.3 113.7 %collective-permute-start.14 = (bf16[512,1024]{1,0:T(8,128)(2,1)}, bf16[512,1024]{1,0:T(8,128)(2,1)}, u32[]{:S(2)}, u32[]{:S(2)}) collective-permute-start(bf16[512,1024]{1,0:T(8,128)(2,1)} %attend.4), channel_id=1, source_target_pairs={{0,1},{1,0},{2,3},{3,2},{4,5},{5,4},{6,7},{7,6},{8,9},{9,8},{10,11... | collective-permute-start | bytes 3145736 | tf_op jit(solution)/shard_map/ppermute | solution.py:234
  78.6 77.2 %collective-permute-start.16 = (bf16[1440,256]{1,0:T(8,128)(2,1)}, bf16[1440,256]{1,0:T(8,128)(2,1)}, u32[]{:S(2)}, u32[]{:S(2)}) collective-permute-start(bf16[1440,256]{1,0:T(8,128)(2,1)} %collective-permute-done.4.rest_2_.refs_1_), channel_id=1, source_target_pairs={{0,8},{1,9},{2,10},{3,11},{4,12},{5,13},{6,14},{7,15},{8,0},{9,1},... | collective-permute-start | bytes 2211848 | tf_op jit(solution)/shard_map/ppermute | solution.py:234
  91.3 64.5 %collective-permute-start.17 = (bf16[1440,256]{1,0:T(8,128)(2,1)}, bf16[1440,256]{1,0:T(8,128)(2,1)}, u32[]{:S(2)}, u32[]{:S(2)}) collective-permute-start(bf16[1440,256]{1,0:T(8,128)(2,1)} %collective-permute-done.4.rest_2_.refs_1_), channel_id=1, source_target_pairs={{0,16},{1,17},{2,18},{3,19},{4,20},{5,21},{6,22},{7,23},{8,24},{9,... | collective-permute-start | bytes 2211848 | tf_op jit(solution)/shard_map/ppermute | solution.py:234
  91.4 65.0 %collective-permute-start.22 = (bf16[1440,256]{1,0:T(8,128)(2,1)}, bf16[1440,256]{1,0:T(8,128)(2,1)}, u32[]{:S(2)}, u32[]{:S(2)}) collective-permute-start(bf16[1440,256]{1,0:T(8,128)(2,1)} %collective-permute-done.20.refs_6_), channel_id=1, source_target_pairs={{0,16},{1,17},{2,18},{3,19},{4,20},{5,21},{6,22},{7,23},{8,24},{9,... | collective-permute-start | bytes 2211848 | tf_op jit(solution)/shard_map/ppermute | solution.py:234
  92.9 84.2 %collective-permute-start.15 = (bf16[512,1024]{1,0:T(8,128)(2,1)}, bf16[512,1024]{1,0:T(8,128)(2,1)}, u32[]{:S(2)}, u32[]{:S(2)}) collective-permute-start(bf16[512,1024]{1,0:T(8,128)(2,1)} %attend.5), channel_id=1, source_target_pairs={{0,1},{1,0},{2,3},{3,2},{4,5},{5,4},{6,7},{7,6},{8,9},{9,8},{10,11... | collective-permute-start | bytes 3145736 | tf_op jit(solution)/shard_map/ppermute | solution.py:234
  155.8 22.1 %collective-permute-start.12 = (bf16[512,1024]{1,0:T(8,128)(2,1)}, bf16[512,1024]{1,0:T(8,128)(2,1)S(1)}, u32[]{:S(2)}, u32[]{:S(2)}) collective-permute-start(bf16[512,1024]{1,0:T(8,128)(2,1)} %attend.6), channel_id=1, source_target_pairs={{0,1},{1,0},{2,3},{3,2},{4,5},{5,4},{6,7},{7,6},{8,9},{9,8},{10,11... | collective-permute-start | bytes 3145736 | tf_op jit(solution)/shard_map/ppermute | solution.py:234
  155.9 22.6 %collective-permute-start.13 = (bf16[512,1024]{1,0:T(8,128)(2,1)}, bf16[512,1024]{1,0:T(8,128)(2,1)}, u32[]{:S(2)}, u32[]{:S(2)}) collective-permute-start(bf16[512,1024]{1,0:T(8,128)(2,1)} %attend.7), channel_id=1, source_target_pairs={{0,1},{1,0},{2,3},{3,2},{4,5},{5,4},{6,7},{7,6},{8,9},{9,8},{10,11... | collective-permute-start | bytes 3145736 | tf_op jit(solution)/shard_map/ppermute | solution.py:234
  156.4 18.3 %collective-permute-start.21 = (bf16[1440,256]{1,0:T(8,128)(2,1)}, bf16[1440,256]{1,0:T(8,128)(2,1)}, u32[]{:S(2)}, u32[]{:S(2)}) collective-permute-start(bf16[1440,256]{1,0:T(8,128)(2,1)} %collective-permute-done.20.refs_6_), channel_id=1, source_target_pairs={{0,8},{1,9},{2,10},{3,11},{4,12},{5,13},{6,14},{7,15},{8,0},{9,1},... | collective-permute-start | bytes 2211848 | tf_op jit(solution)/shard_map/ppermute | solution.py:234
  174.7 26.0 %collective-permute-start.18 = (bf16[768,256]{1,0:T(8,128)(2,1)}, bf16[768,256]{1,0:T(8,128)(2,1)}, u32[]{:S(2)}, u32[]{:S(2)}) collective-permute-start(bf16[768,256]{1,0:T(8,128)(2,1)} %slice.59), channel_id=1, source_target_pairs={{0,8},{1,9},{2,10},{3,11},{4,12},{5,13},{6,14},{7,15},{8,0},{9,1},... | collective-permute-start | bytes 1179656 | tf_op jit(solution)/shard_map/ppermute | solution.py:234
  177.0 33.5 %collective-permute-start.23 = (bf16[768,256]{1,0:T(8,128)(2,1)}, bf16[768,256]{1,0:T(8,128)(2,1)S(1)}, u32[]{:S(2)}, u32[]{:S(2)}) collective-permute-start(bf16[768,256]{1,0:T(8,128)(2,1)} %slice.61), channel_id=1, source_target_pairs={{0,8},{1,9},{2,10},{3,11},{4,12},{5,13},{6,14},{7,15},{8,0},{9,1},... | collective-permute-start | bytes 1179656 | tf_op jit(solution)/shard_map/ppermute | solution.py:234
  177.9 32.6 %collective-permute-start.25 = (bf16[768,256]{1,0:T(8,128)(2,1)}, bf16[768,256]{1,0:T(8,128)(2,1)S(1)}, u32[]{:S(2)}, u32[]{:S(2)}) collective-permute-start(bf16[768,256]{1,0:T(8,128)(2,1)} %slice.63), channel_id=1, source_target_pairs={{0,8},{1,9},{2,10},{3,11},{4,12},{5,13},{6,14},{7,15},{8,0},{9,1},... | collective-permute-start | bytes 1179656 | tf_op jit(solution)/shard_map/ppermute | solution.py:234
  178.5 32.0 %collective-permute-start.24 = (bf16[672,256]{1,0:T(8,128)(2,1)}, bf16[672,256]{1,0:T(8,128)(2,1)}, u32[]{:S(2)}, u32[]{:S(2)}) collective-permute-start(bf16[672,256]{1,0:T(8,128)(2,1)} %slice.62), channel_id=1, source_target_pairs={{0,16},{1,17},{2,18},{3,19},{4,20},{5,21},{6,22},{7,23},{8,24},{9,... | collective-permute-start | bytes 1032200 | tf_op jit(solution)/shard_map/ppermute | solution.py:234
  190.2 20.3 %collective-permute-start.26 = (bf16[672,256]{1,0:T(8,128)(2,1)}, bf16[672,256]{1,0:T(8,128)(2,1)}, u32[]{:S(2)}, u32[]{:S(2)}) collective-permute-start(bf16[672,256]{1,0:T(8,128)(2,1)} %slice.64), channel_id=1, source_target_pairs={{0,16},{1,17},{2,18},{3,19},{4,20},{5,21},{6,22},{7,23},{8,24},{9,... | collective-permute-start | bytes 1032200 | tf_op jit(solution)/shard_map/ppermute | solution.py:234
  (18 other events, 260.5 us)

commit v2 on v1

v2 whole, which is shorter than its diff:
```python
import functools

import jax
import jax.numpy as jnp
from jax import lax
from jax.experimental import pallas as pl
from jax.experimental.pallas import tpu as pltpu
from jax.sharding import PartitionSpec as P

KVH = 8
HD = 64
BLK = 128
MASKED = -1e30
TRUSTED = 1e26
AXES = ("gx", "gy")
VMEM_LIMIT = 60 * 1024 * 1024


def contract_last(a, b):
    return lax.dot_general(a, b, (((1,), (1,)), ((), ())), preferred_element_type=jnp.float32)


def dot(a, b):
    return jnp.dot(a, b, preferred_element_type=jnp.float32)


def attend_kernel(chained, first, scal, *refs):
    here, there = refs[0:6], refs[6:12]
    sink_ref = refs[12]
    big_ref, piece_ref, kx, vx, qx, worst = refs[13 + chained :]
    block = pl.program_id(0) + first
    use_here = scal[3] > 0
    cache_rows, tree_rows = here[1].shape[0], here[3].shape[0]
    key_rows = cache_rows + tree_rows
    pairs = here[0].shape[1] // BLK // 2
    node_total = jnp.where(use_here, scal[1], scal[4])
    cache_total = jnp.where(use_here, scal[2], scal[5])

    def chosen(source):
        _, kc_ref, vc_ref, kt_ref, vt_ref, _ = source
        kx[0:cache_rows, 0:BLK] = kc_ref[...]
        kx[cache_rows:key_rows, 0:BLK] = kt_ref[...]
        vx[0:cache_rows, 0:BLK] = vc_ref[...]
        vx[cache_rows:key_rows, 0:BLK] = vt_ref[...]

    @pl.when(block == first)
    def _():
        @pl.when(use_here)
        def _():
            chosen(here)

        @pl.when(jnp.logical_not(use_here))
        def _():
            chosen(there)

        vx[:, BLK : 2 * BLK] = jnp.ones((key_rows, BLK), jnp.bfloat16)
        row = lax.broadcasted_iota(jnp.int32, (cache_rows, BLK), 0)
        kx[0:cache_rows, BLK : 2 * BLK] = jnp.where(row < cache_total, 0.0, MASKED).astype(jnp.bfloat16)
        src = lax.broadcasted_iota(jnp.int32, (BLK, BLK), 0)
        dst = lax.broadcasted_iota(jnp.int32, (BLK, BLK), 1)
        own = jnp.where(src == dst, 1.0, 0.0).astype(jnp.bfloat16)
        for at in range(qx.shape[0]):
            qx[at, 0:BLK, BLK : 2 * BLK] = own
            qx[at, BLK : 2 * BLK, BLK : 2 * BLK] = own

    live = block * BLK < node_total

    @pl.when(live)
    def _():
        lane = lax.broadcasted_iota(jnp.int32, (BLK, BLK), 1)
        low = lane < HD
        node = lax.broadcasted_iota(jnp.int32, (BLK, BLK), 0) + block * BLK
        top = lax.broadcasted_iota(jnp.int32, (2 * BLK, 1), 0) < BLK
        zero = jnp.zeros((BLK, BLK), jnp.float32)
        kx[cache_rows:key_rows, BLK : 2 * BLK] = jnp.where(use_here, here[5][...], there[5][...])

        def queries(head, pair):
            cols = pl.ds(pl.multiple_of((head * pairs + pair) * BLK, BLK), BLK)
            both = jnp.where(use_here, here[0][:, cols], there[0][:, cols]).astype(jnp.float32) * (HD**-0.5)
            turned = pltpu.roll(both, HD, 1)
            if head == 0:
                first, second = jnp.where(low, both, zero), jnp.where(low, turned, zero)
            else:
                first, second = jnp.where(low, zero, turned), jnp.where(low, zero, both)
            qx[head, 0:BLK, 0:BLK] = first.astype(jnp.bfloat16)
            qx[head, BLK : 2 * BLK, 0:BLK] = second.astype(jnp.bfloat16)
            return qx[head]

        def sink_of(head, pair, kind):
            at = 2 * (head * pairs + pair)
            return jnp.where(top, sink_ref[kind, at], sink_ref[kind, at + 1])

        def store(head, pair, result):
            first, second = result[0:BLK], result[BLK : 2 * BLK]
            if head == 0:
                joined = jnp.where(low, first, pltpu.roll(second, HD, 1))
            else:
                joined = jnp.where(low, pltpu.roll(first, HD, 1), second)
            joined = jnp.where(node < node_total, joined, zero).astype(jnp.bfloat16)
            cols = pl.ds(pl.multiple_of((head * pairs + pair) * BLK, BLK), BLK)
            big_ref[:, cols] = joined
            piece_ref[:, cols] = joined

        worst[...] = zero

        def quick(pair, carry):
            for head in (0, 1):
                scores = contract_last(queries(head, pair), kx[...])
                weights = jnp.exp(scores).astype(jnp.bfloat16)
                sums = dot(weights, vx[...])
                under = sums[:, BLK : 2 * BLK] + sink_of(head, pair, 1)
                worst[...] = jnp.maximum(worst[...], jnp.maximum(under[0:BLK], under[BLK : 2 * BLK]))
                store(head, pair, sums[:, 0:BLK] / under)
            return carry

        lax.fori_loop(0, pairs, quick, 0)

        @pl.when(jnp.logical_not(jnp.max(worst[...]) < TRUSTED))
        def _():
            def careful(pair, carry):
                for head in (0, 1):
                    scores = contract_last(queries(head, pair), kx[...])
                    sink = sink_of(head, pair, 0)
                    peak = jnp.maximum(jnp.max(scores, axis=1, keepdims=True), sink)
                    weights = jnp.exp(scores - peak).astype(jnp.bfloat16)
                    sums = dot(weights, vx[...])
                    under = sums[:, BLK : 2 * BLK] + jnp.exp(sink - peak)
                    store(head, pair, sums[:, 0:BLK] / under)
                return carry

            lax.fori_loop(0, pairs, careful, 0)

    @pl.when(jnp.logical_not(live))
    def _():
        big_ref[...] = jnp.zeros_like(big_ref)
        piece_ref[...] = jnp.zeros_like(piece_ref)


def attend(scal, here, there, sinks, at, first, count, rows, tree_rows, before):
    q, k_cache, _, k_tree, _, _ = here
    q_got, kv_got, bias_got = there
    cache_rows = k_cache.shape[0]
    width = q.shape[1] // (KVH // 2)
    full_tree = k_tree.shape[0]
    first_tree = 2 * cache_rows // tree_rows
    second_tree = (2 * cache_rows + full_tree) // tree_rows
    keys = cache_rows + tree_rows
    per_core = KVH // 4

    def mine(s):
        return s[0] * per_core + at

    in_specs = [
        pl.BlockSpec((BLK, width), lambda i, s: (first + i, mine(s))),
        *[pl.BlockSpec((cache_rows, BLK), lambda i, s: (0, mine(s)))] * 2,
        *[pl.BlockSpec((tree_rows, BLK), lambda i, s: (0, mine(s)))] * 2,
        pl.BlockSpec((tree_rows, BLK), lambda i, s: (0, first + i)),
        pl.BlockSpec((BLK, width), lambda i, s: (first + i, at)),
        pl.BlockSpec((cache_rows, BLK), lambda i, s: (0, at)),
        pl.BlockSpec((cache_rows, BLK), lambda i, s: (1, at)),
        pl.BlockSpec((tree_rows, BLK), lambda i, s: (first_tree, at)),
        pl.BlockSpec((tree_rows, BLK), lambda i, s: (second_tree, at)),
        pl.BlockSpec((tree_rows, BLK), lambda i, s: (0, first + i)),
        pl.BlockSpec(memory_space=pltpu.SMEM),
    ]
    operands = [*here, q_got, kv_got, kv_got, kv_got, kv_got, bias_got, sinks]
    aliases = {}
    for out, array in enumerate(before):
        if array is not None:
            aliases[1 + len(operands)] = out
            in_specs.append(pl.BlockSpec(memory_space=pl.ANY))
            operands.append(array)
    heads = width // HD
    work = count * BLK * heads * keys
    return pl.pallas_call(
        functools.partial(attend_kernel, len(aliases), first),
        grid_spec=pltpu.PrefetchScalarGridSpec(
            num_scalar_prefetch=1,
            grid=(count,),
            in_specs=in_specs,
            out_specs=[
                pl.BlockSpec((BLK, width), lambda i, s: (first + i, mine(s))),
                pl.BlockSpec((BLK, width), lambda i, s: (first + i, 0)),
            ],
            scratch_shapes=[
                pltpu.VMEM((keys, 2 * BLK), jnp.bfloat16),
                pltpu.VMEM((keys, 2 * BLK), jnp.bfloat16),
                pltpu.VMEM((2, 2 * BLK, 2 * BLK), jnp.bfloat16),
                pltpu.VMEM((BLK, BLK), jnp.float32),
            ],
        ),
        out_shape=[
            jax.ShapeDtypeStruct((rows, q.shape[1]), jnp.bfloat16),
            jax.ShapeDtypeStruct((rows, width), jnp.bfloat16),
        ],
        input_output_aliases=aliases,
        compiler_params=pltpu.CompilerParams(vmem_limit_bytes=VMEM_LIMIT),
        cost_estimate=pl.CostEstimate(
            flops=work * 2 * 4 * BLK, bytes_accessed=8 * keys * BLK, transcendentals=work
        ),
        name="attend",
    )(scal, *operands)


def tree_bias(words_t, key_total):
    spread = jnp.repeat(words_t, 32, axis=0)
    shift = (jnp.arange(key_total, dtype=jnp.int32) % 32)[:, None]
    flag = jnp.bitwise_and(lax.shift_right_logical(spread, jnp.broadcast_to(shift, spread.shape)), 1)
    return jnp.where(flag > 0, 0.0, MASKED).astype(jnp.bfloat16)


def project_kernel(slots, last, has_acc, info, *refs):
    refs = list(refs)
    n = len(slots)
    busy, light, blocks = refs[:n], refs[n : 2 * n], refs[2 * n : 3 * n]
    refs = refs[3 * n :]
    part = None
    for x in range(n):
        rows = jnp.concatenate([busy[x][...], light[x][...]], axis=0)
        term = contract_last(blocks[x][...], rows)
        part = term if part is None else part + term
    if has_acc:
        part = part + refs.pop(0)[...]
    if not last:
        refs[0][...] = part
        return
    own_ref, other_ref = refs
    done = part.astype(jnp.bfloat16)
    nodes = busy[0].shape[0]
    few = light[0].shape[0]
    rest = jnp.zeros((done.shape[0], nodes - few), jnp.bfloat16)

    @pl.when(info[0] > 0)
    def _():
        own_ref[...] = done[:, :nodes]
        other_ref[:, 0:few] = done[:, nodes:]
        other_ref[:, few:] = rest

    @pl.when(info[0] <= 0)
    def _():
        other_ref[...] = done[:, :nodes]
        own_ref[:, 0:few] = done[:, nodes:]
        own_ref[:, few:] = rest


def project(info, busy, light, acc, blocks, slots, last):
    columns, depth = blocks[0].shape
    tile = columns // 6
    rows = busy.shape[0] + light.shape[0]
    n = len(slots)

    def at_slot(rows_of, slot):
        return pl.BlockSpec((rows_of, depth), lambda i, s: (0, s[slot]))

    in_specs = [at_slot(busy.shape[0], slot) for slot in slots]
    in_specs += [at_slot(light.shape[0], slot) for slot in slots]
    in_specs += [pl.BlockSpec((tile, depth), lambda i, s: (i, 0))] * n
    operands = [busy] * n + [light] * n + list(blocks)
    if acc is not None:
        in_specs.append(pl.BlockSpec((tile, rows), lambda i, s: (i, 0)))
        operands.append(acc)
    if last:
        out_specs = [
            pl.BlockSpec((tile, busy.shape[0]), lambda i, s: (s[1] * 6 + i, 0)),
            pl.BlockSpec((tile, busy.shape[0]), lambda i, s: (i, 0)),
        ]
        out_shape = [
            jax.ShapeDtypeStruct((2 * columns, busy.shape[0]), jnp.bfloat16),
            jax.ShapeDtypeStruct((columns, busy.shape[0]), jnp.bfloat16),
        ]
    else:
        out_specs = pl.BlockSpec((tile, rows), lambda i, s: (i, 0))
        out_shape = jax.ShapeDtypeStruct((columns, rows), jnp.float32)
    return pl.pallas_call(
        functools.partial(project_kernel, slots, last, acc is not None),
        grid_spec=pltpu.PrefetchScalarGridSpec(
            num_scalar_prefetch=1, grid=(6,), in_specs=in_specs, out_specs=out_specs
        ),
        out_shape=out_shape,
        compiler_params=pltpu.CompilerParams(vmem_limit_bytes=VMEM_LIMIT),
        cost_estimate=pl.CostEstimate(
            flops=2 * rows * columns * depth * n, bytes_accessed=rows * columns * 8, transcendentals=0
        ),
        name="project",
    )(info, *operands)


def on_device(plane, line, args):
    (
        q_nodes, k_cache, v_cache, k_tree, v_tree, anc_bits, node_count, cache_len, sinks, o_weight,
    ) = args
    gx = lax.axis_index("gx")
    gy = lax.axis_index("gy")
    core = gy % 2
    far = 1 - core
    z = gy // 2
    is_busy = (gx + gy) % 2 == 0
    places = [(a, b, c) for a in range(plane) for b in range(line) for c in range(2)]

    def number(a, b, c):
        return (a * line + b) * 2 + c

    def moved(x, to):
        pairs = [(number(*p), number(*to(*p))) for p in places]
        return lax.ppermute(x, AXES, pairs)

    def swapped(x):
        return moved(x, lambda a, b, c: (a, b, 1 - c))

    q, kc, vc, kt, vt = q_nodes[0], k_cache[0], v_cache[0], k_tree[0], v_tree[0]
    node_total = q.shape[0]
    tree_rows = kt.shape[0]
    columns = o_weight.shape[1] // 2
    half_q, half_kv = q.shape[1] // 2, kc.shape[1] // 2

    w_t = o_weight.T
    w_mine = lax.dynamic_slice_in_dim(w_t, core * columns, columns, 0)
    w_theirs = swapped(lax.dynamic_slice_in_dim(w_t, far * columns, columns, 0))
    b0 = jnp.where(
        core == 0,
        jnp.concatenate([w_mine, w_theirs], axis=1),
        jnp.concatenate([w_theirs, w_mine], axis=1),
    )

    words_t = anc_bits[0].T
    counts = jnp.concatenate([node_count, cache_len])
    note = jnp.concatenate([words_t, jnp.broadcast_to(counts[:, None], (2, node_total))], axis=0)
    q_away = lax.dynamic_slice_in_dim(q, far * half_q, half_q, 1)
    kv_away = jnp.concatenate(
        [lax.dynamic_slice_in_dim(a, far * half_kv, half_kv, 1) for a in (kc, vc, kt, vt)], axis=0
    )
    q_got, kv_got, note_got = swapped(q_away), swapped(kv_away), swapped(note)
    words = words_t.shape[0]
    here = (q, kc, vc, kt, vt, tree_bias(words_t, tree_rows))
    there = (q_got, kv_got, tree_bias(note_got[:words], tree_rows))
    numbers = [node_count[0], cache_len[0], note_got[words, 0], note_got[words + 1, 0]]

    def scalars(use_here):
        flag = use_here.astype(jnp.int32)
        return jnp.stack([core, numbers[0], numbers[1], flag, numbers[2], numbers[3]]).astype(jnp.int32)

    per_pair = sinks.shape[0] // 4
    sink_table = jnp.stack([sinks, jnp.exp(sinks)])

    def pair_sinks(at):
        return lax.dynamic_slice_in_dim(sink_table, (core * 2 + at) * per_pair, per_pair, 1)

    half = node_total // BLK // 2

    def attend_busy(at, first, before):
        flags = scalars(is_busy)
        return attend(
            flags, here, there, pair_sinks(at), at, first, half, node_total, tree_rows, before
        )

    def attend_light(at, big):
        flags = scalars(jnp.logical_not(is_busy))
        return attend(flags, here, there, pair_sinks(at), at, 0, 1, BLK, BLK, (big, None))

    direct = plane == 4 and line == 4

    def along_x(x):
        return moved(x, lambda a, b, c: (a ^ 1, b, c))

    def along_y(x):
        return moved(x, lambda a, b, c: (a ^ 2, b, c))

    def along_z(x, by):
        return moved(x, lambda a, b, c: (a, (b + by) % line, c))

    def together(*arrays):
        return lax.optimization_barrier(arrays) if direct else arrays

    if direct:
        x0, y0, z1 = along_x(b0), along_y(b0), along_z(b0, 1)
    else:
        x0 = y0 = z1 = b0
    busy, busy0 = attend_busy(0, 0, (None, None))
    busy, busy0, b0, x0, y0, z1 = together(busy, busy0, b0, x0, y0, z1)
    if direct:
        d0, y1, z3 = along_x(y0), along_y(z1), along_z(b0, 3)
        x1, z2 = along_x(z1), along_z(z1, 1)
    else:
        d0 = y1 = z3 = x1 = z2 = b0
    busy, busy0 = attend_busy(0, half, (busy, busy0))
    busy, busy0, d0, y1, z3 = together(busy, busy0, d0, y1, z3)
    if direct:
        y3, d1, d3 = along_y(z3), along_z(d0, 1), along_z(d0, 3)
    else:
        y3 = d1 = d3 = b0
    busy, busy1 = attend_busy(1, 0, (busy, None))
    busy, busy1, x1, z2, z3 = together(busy, busy1, x1, z2, z3)
    if direct:
        x2, y2, x3 = along_x(z2), along_y(z2), along_x(z3)
    else:
        x2 = y2 = x3 = b0
    busy, busy1 = attend_busy(1, half, (busy, busy1))
    busy, busy1, x2 = together(busy, busy1, x2)
    d2 = along_y(x2) if direct else b0
    light, light0 = attend_light(0, None)
    light, light1 = attend_light(1, light)
    for at, (piece_b, piece_l) in enumerate(((busy0, light0), (busy1, light1))):
        col = (far * 2 + at) * busy0.shape[1]
        busy = lax.dynamic_update_slice(busy, swapped(piece_b), (0, col))
        light = lax.dynamic_update_slice(light, swapped(piece_l), (0, col))

    padded = jnp.concatenate([light, jnp.zeros((node_total - BLK, light.shape[1]), light.dtype)], axis=0)
    attended = jnp.where(is_busy, busy, padded)

    if direct:
        slots = {}
        info = [is_busy.astype(jnp.int32), core]
        for dz in (0, 1, 3, 2):
            for flip in (0, 1, 2, 3):
                slots[(dz, flip)] = len(info)
                info.append((gx ^ flip) * line + (z - dz) % line)
        info = jnp.stack(info).astype(jnp.int32)

        def stage(acc, blocks, last):
            return project(
                info, busy, light, acc, [b for b, _ in blocks], tuple(slots[k] for _, k in blocks), last
            )

        blocks = [
            (b0, (0, 0)), (x0, (0, 1)), (y0, (0, 2)), (d0, (0, 3)),
            (z1, (1, 0)), (x1, (1, 1)), (y1, (1, 2)), (d1, (1, 3)),
            (z3, (3, 0)), (x3, (3, 1)), (y3, (3, 2)), (d3, (3, 3)),
            (z2, (2, 0)), (x2, (2, 1)), (y2, (2, 2)), (d2, (2, 3)),
        ]
        full, other_half = stage(None, blocks, True)
        full = lax.dynamic_update_slice(full, swapped(other_half), (far * columns, 0))
        projected = full.T
    else:
        w_all = lax.all_gather(o_weight, AXES, axis=0, tiled=True)
        projected = dot(attended, w_all).astype(jnp.bfloat16)
    return attended[None], projected[None]


def solution(mesh):
    plane, line = mesh.shape["gx"], mesh.shape["gy"] // 2
    rows = P(AXES, None, None)
    placed = (rows, rows, rows, rows, rows, rows, P(AXES), P(AXES), P(), P(AXES, None))

    def run(*args):
        return on_device(plane, line, args)

    return jax.shard_map(run, mesh=mesh, in_specs=placed, out_specs=(rows, rows), check_vma=False)
```

time: 244 us -> 243 us (level)
  the two profiles are of different devices: /device:TPU:9 before, /device:TPU:0 now
where the time goes in v2:
time: 243 us
  Pallas kernels  151 us (62%)
  waiting for transfers between devices  43.6 us (18%)
  starting transfers between devices  21 us (9%)
  local copies, waits for them, and re-layouts  16.7 us (7%)
  other arithmetic  8.66 us (4%)
    pallas_call x6, Pallas kernels, attend(): pl.pallas_call(functools.partial(attend_kernel, len(aliases), first), gri...  133 us
    ppermute x24, waiting for transfers between devices, moved(): return lax.ppermute(x, AXES, pairs)  43.6 us
    ppermute x24, starting transfers between devices, moved(): return lax.ppermute(x, AXES, pairs)  21 us
    pallas_call x1, Pallas kernels, project(): pl.pallas_call(functools.partial(project_kernel, slots, last, acc is not...  17.7 us
    broadcast_in_dim x1, other arithmetic, on_device(): return (attended[None], projected[None])  5.61 us
  transfers between devices with their start and end apart: 24, of which 7 were waited for; matrix products, arithmetic and copies ran while one was open for 7% of the time, Pallas kernels for 55%

profile of v2, /device:TPU:0, one launch (start us, length us, event | category | flops | bytes accessed | tf_op | source)
XLA Modules:
  0.0 243.0 jit_solution(16710998197673750341)
XLA Ops:
  0.7 3.3 %dynamic-slice_bitcast_fusion = bf16[512,2048]{1,0:T(8,128)(2,1)} fusion(bf16[1,512,4096]{2,1,0:T(8,128)(2,1)} %param.10, s32[]{:T(128)S(6)} %select_n.129), kind=kLoop, calls=%fused_computation.1 | loop fusion | bytes 4194308 | tf_op jit(solution)/shard_map/dynamic_slice | solution.py:328
  8.2 3.2 %collective-permute-done.3 = bf16[1440,128]{1,0:T(8,128)(2,1)S(1)} collective-permute-done((bf16[1440,128]{1,0:T(8,128)(2,1)S(1)}, bf16[1440,128]{1,0:T(8,128)(2,1)S(1)}, u32[]{:S(2)}, u32[]{:S(2)}) %collective-permute-start.3) | collective-permute-done | bytes 368672 | tf_op jit(solution)/shard_map/ppermute | solution.py:305
  11.6 2.9 %collective-permute-start.4 = (bf16[1440,256]{1,0:T(8,128)(2,1)S(1)}, bf16[1440,256]{1,0:T(8,128)(2,1)S(1)}, u32[]{:S(2)}, u32[]{:S(2)}) collective-permute-start(bf16[1440,256]{1,0:T(8,128)(2,1)S(1)} %maximum_select_fusion.refs_32_), channel_id=1, source_target_pairs={{0,8},{1,9},{2,10},{3,11},{4,12},{5,13},{6,14},{7,15},{8,0},{9,1},... | collective-permute-start | bytes 2211848 | tf_op jit(solution)/shard_map/ppermute | solution.py:305
  14.5 1.5 collective-permute-start.5
  16.1 1.6 collective-permute-start.6
  20.3 1.9 stack.99.scal
  23.3 26.6 %attend.6 = (bf16[512,4096]{1,0:T(8,128)(2,1)}, bf16[512,1024]{1,0:T(8,128)(2,1)}) custom-call(s32[6]{0:T(128)} %stack.99.scal, bf16[512,4096]{1,0:T(8,128)(2,1)} %bitcast.67, bf16[1024,512]{1,0:T(8,128)(2,1)} %bitcast.73, bf16[1024,512]{1,0:T(8,128)(2,1)} %bitcast.79, bf16[512,512]{1,0:T(8,128)(2,1)} %bitcast.85, bf16[512,512]{1,0:T(8,128)(2,1)} %bitcast.91, ...), custom_call_target="tpu_custom_call" | custom-call | flops 6442450944 | bytes 1572864 | tf_op jit(solution)/shard_map/attend/pallas_call | solution.py:175
  51.1 2.0 collective-permute-start.9
  53.2 1.7 collective-permute-start.10
  54.9 26.7 %attend.7 = (bf16[512,4096]{1,0:T(8,128)(2,1)}, bf16[512,1024]{1,0:T(8,128)(2,1)}) custom-call(s32[6]{0:T(128)} %stack.99.scal, bf16[512,4096]{1,0:T(8,128)(2,1)} %bitcast.68, bf16[1024,512]{1,0:T(8,128)(2,1)} %bitcast.74, bf16[1024,512]{1,0:T(8,128)(2,1)} %bitcast.80, bf16[512,512]{1,0:T(8,128)(2,1)} %bitcast.86, ...), custom_call_target="tpu_custom_call", output_to_operand_aliasing={{0}: (14, {}), {1}: (15, {})} | custom-call | flops 6442450944 | bytes 1572864 | tf_op jit(solution)/shard_map/attend/pallas_call | solution.py:175
  81.6 26.7 %attend.8 = (bf16[512,4096]{1,0:T(8,128)(2,1)}, bf16[512,1024]{1,0:T(8,128)(2,1)}) custom-call(s32[6]{0:T(128)} %stack.99.scal, bf16[512,4096]{1,0:T(8,128)(2,1)} %bitcast.69, bf16[1024,512]{1,0:T(8,128)(2,1)} %bitcast.75, bf16[1024,512]{1,0:T(8,128)(2,1)} %bitcast.81, bf16[512,512]{1,0:T(8,128)(2,1)} %bitcast.87, ...), custom_call_target="tpu_custom_call", output_to_operand_aliasing={{0}: (14, {})} | custom-call | flops 6442450944 | bytes 1572864 | tf_op jit(solution)/shard_map/attend/pallas_call | solution.py:175
  108.7 26.6 %attend.9 = (bf16[512,4096]{1,0:T(8,128)(2,1)}, bf16[512,1024]{1,0:T(8,128)(2,1)}) custom-call(s32[6]{0:T(128)} %stack.99.scal, bf16[512,4096]{1,0:T(8,128)(2,1)} %bitcast.70, bf16[1024,512]{1,0:T(8,128)(2,1)} %bitcast.76, bf16[1024,512]{1,0:T(8,128)(2,1)} %bitcast.82, bf16[512,512]{1,0:T(8,128)(2,1)} %bitcast.88, ...), custom_call_target="tpu_custom_call", output_to_operand_aliasing={{0}: (14, {}), {1}: (15, {})} | custom-call | flops 6442450944 | bytes 1572864 | tf_op jit(solution)/shard_map/attend/pallas_call | solution.py:175
  136.7 1.7 collective-permute-start.18
  138.4 2.0 stack.105.scal
  140.4 13.3 %attend.10 = (bf16[128,4096]{1,0:T(8,128)(2,1)}, bf16[128,1024]{1,0:T(8,128)(2,1)}) custom-call(s32[6]{0:T(128)} %stack.105.scal, bf16[512,4096]{1,0:T(8,128)(2,1)} %bitcast.71, bf16[1024,512]{1,0:T(8,128)(2,1)} %bitcast.77, bf16[1024,512]{1,0:T(8,128)(2,1)} %bitcast.83, bf16[512,512]{1,0:T(8,128)(2,1)} %bitcast.89, bf16[512,512]{1,0:T(8,128)(2,1)} %bitcast.95, ...), custom_call_target="tpu_custom_call" | custom-call | flops 2415919104 | bytes 1179648 | tf_op jit(solution)/shard_map/attend/pallas_call | solution.py:175
  153.7 13.2 %attend.11 = (bf16[128,4096]{1,0:T(8,128)(2,1)}, bf16[128,1024]{1,0:T(8,128)(2,1)}) custom-call(s32[6]{0:T(128)} %stack.105.scal, bf16[512,4096]{1,0:T(8,128)(2,1)} %bitcast.72, bf16[1024,512]{1,0:T(8,128)(2,1)} %bitcast.78, bf16[1024,512]{1,0:T(8,128)(2,1)} %bitcast.84, bf16[512,512]{1,0:T(8,128)(2,1)} %bitcast.90, ...), custom_call_target="tpu_custom_call", output_to_operand_aliasing={{0}: (14, {})} | custom-call | flops 2415919104 | bytes 1179648 | tf_op jit(solution)/shard_map/attend/pallas_call | solution.py:175
  169.5 3.8 %collective-permute-start.20 = (bf16[1440,256]{1,0:T(8,128)(2,1)S(1)}, bf16[1440,256]{1,0:T(8,128)(2,1)}, u32[]{:S(2)}, u32[]{:S(2)}) collective-permute-start(bf16[1440,256]{1,0:T(8,128)(2,1)S(1)} %copy-done.9), channel_id=1, source_target_pairs={{0,6},{1,7},{2,0},{3,1},{4,2},{5,3},{6,4},{7,5},{8,14},{9,15},{10,... | collective-permute-start | bytes 2211848 | tf_op jit(solution)/shard_map/ppermute | solution.py:305
  178.8 8.3 %collective-permute-done.21.refs_46_ = bf16[1440,256]{1,0:T(8,128)(2,1)} collective-permute-done((bf16[1440,256]{1,0:T(8,128)(2,1)}, bf16[1440,256]{1,0:T(8,128)(2,1)}, u32[]{:S(2)}, u32[]{:S(2)}) %collective-permute-start.21) | collective-permute-done | bytes 737312 | tf_op jit(solution)/shard_map/ppermute | solution.py:305
  187.1 3.7 %collective-permute-done.17.refs_39_ = bf16[1440,256]{1,0:T(8,128)(2,1)} collective-permute-done((bf16[1440,256]{1,0:T(8,128)(2,1)S(1)}, bf16[1440,256]{1,0:T(8,128)(2,1)}, u32[]{:S(2)}, u32[]{:S(2)}) %collective-permute-start.17) | collective-permute-done | bytes 737312 | tf_op jit(solution)/shard_map/ppermute | solution.py:305
  190.8 12.1 %collective-permute-done.19.refs_42_ = bf16[1440,256]{1,0:T(8,128)(2,1)} collective-permute-done((bf16[1440,256]{1,0:T(8,128)(2,1)}, bf16[1440,256]{1,0:T(8,128)(2,1)}, u32[]{:S(2)}, u32[]{:S(2)}) %collective-permute-start.19) | collective-permute-done | bytes 737312 | tf_op jit(solution)/shard_map/ppermute | solution.py:305
  204.2 13.6 %collective-permute-done.22.refs_47_ = bf16[1440,256]{1,0:T(8,128)(2,1)} collective-permute-done((bf16[1440,256]{1,0:T(8,128)(2,1)}, bf16[1440,256]{1,0:T(8,128)(2,1)}, u32[]{:S(2)}, u32[]{:S(2)}) %collective-permute-start.22) | collective-permute-done | bytes 737312 | tf_op jit(solution)/shard_map/ppermute | solution.py:305
  217.8 17.7 %project.1 = (bf16[2880,512]{1,0:T(8,128)(2,1)}, bf16[1440,512]{1,0:T(8,128)(2,1)}) custom-call(s32[18]{0:T(128)} %stack.122.info, bf16[512,4096]{1,0:T(8,128)(2,1)} %constant_dynamic-update-slice_fusion.3.refs_0_.refs_1_.refs_2_.refs_3_.refs_4_.refs_5_.refs_6_.refs_7_.refs_8_.refs_9_.refs_10_.refs_11_.refs_12_.refs_13_.refs_14_.refs_15_, ...), custom_call_target="tpu_custom_call" | custom-call | flops 7549747200 | bytes 7372800 | tf_op jit(solution)/shard_map/project/pallas_call | solution.py:274
  235.6 5.6 %select_bitcast_fusion = bf16[1,512,4096]{2,1,0:T(8,128)(2,1)} fusion(bf16[512,4096]{1,0:T(8,128)(2,1)} %constant_dynamic-update-slice_fusion.3.refs_0_.refs_1_.refs_2_.refs_3_.refs_4_.refs_5_.refs_6_.refs_7_.refs_8_.refs_9_.refs_10_.refs_11_.refs_12_.refs_13_.refs_14_.refs_15_, bf16[128,4096]{1,0:T(8,128)(2,1)S(1)} %copy-done, pred[]{:T(512)S(6)} %eq.28), kind=kLoop, calls=%fused_computation | loop fusion | flops 2097152 | bytes 9437185 | tf_op jit(solution)/shard_map/broadcast_in_dim | solution.py:436
  241.4 1.6 copy-done.16
  (90 shorter events, 19.4 us)
Async XLA Ops:
  4.0 18.2 %collective-permute-start.1 = (bf16[512,2048]{1,0:T(8,128)(2,1)}, bf16[512,2048]{1,0:T(8,128)(2,1)}, u32[]{:S(2)}, u32[]{:S(2)}) collective-permute-start(bf16[512,2048]{1,0:T(8,128)(2,1)} %dynamic-slice_bitcast_fusion), channel_id=1, source_target_pairs={{0,1},{1,0},{2,3},{3,2},{4,5},{5,4},{6,7},{7,6},{8,9},{9,8},{10,11... | collective-permute-start | bytes 6291464 | tf_op jit(solution)/shard_map/ppermute | solution.py:305
  5.9 16.3 %collective-permute-start.2 = (bf16[3072,256]{1,0:T(8,128)(2,1)}, bf16[3072,256]{1,0:T(8,128)(2,1)S(1)}, u32[]{:S(2)}, u32[]{:S(2)}) collective-permute-start(bf16[3072,256]{1,0:T(8,128)(2,1)} %pad_maximum_fusion), channel_id=1, source_target_pairs={{0,1},{1,0},{2,3},{3,2},{4,5},{5,4},{6,7},{7,6},{8,9},{9,8},{10,11... | collective-permute-start | bytes 4718600 | tf_op jit(solution)/shard_map/ppermute | solution.py:305
  7.5 8.6 %collective-permute-start = (s32[18,512]{1,0:T(8,128)S(1)}, s32[18,512]{1,0:T(8,128)S(1)}, u32[]{:S(2)}, u32[]{:S(2)}) collective-permute-start(s32[18,512]{1,0:T(8,128)S(1)} %pad_add_fusion), channel_id=1, source_target_pairs={{0,1},{1,0},{2,3},{3,2},{4,5},{5,4},{6,7},{7,6},{8,9},{9,8},{10,11... | collective-permute-start | bytes 110600 | tf_op jit(solution)/shard_map/ppermute | solution.py:305
  8.0 3.3 %collective-permute-start.3 = (bf16[1440,128]{1,0:T(8,128)(2,1)S(1)}, bf16[1440,128]{1,0:T(8,128)(2,1)S(1)}, u32[]{:S(2)}, u32[]{:S(2)}) collective-permute-start(bf16[1440,128]{1,0:T(8,128)(2,1)S(1)} %get-tuple-element.69), channel_id=1, source_target_pairs={{0,1},{1,0},{2,3},{3,2},{4,5},{5,4},{6,7},{7,6},{8,9},{9,8},{10,11... | collective-permute-start | bytes 1105928 | tf_op jit(solution)/shard_map/ppermute | solution.py:305
  11.6 38.4 %collective-permute-start.4 = (bf16[1440,256]{1,0:T(8,128)(2,1)S(1)}, bf16[1440,256]{1,0:T(8,128)(2,1)S(1)}, u32[]{:S(2)}, u32[]{:S(2)}) collective-permute-start(bf16[1440,256]{1,0:T(8,128)(2,1)S(1)} %maximum_select_fusion.refs_32_), channel_id=1, source_target_pairs={{0,8},{1,9},{2,10},{3,11},{4,12},{5,13},{6,14},{7,15},{8,0},{9,1},... | collective-permute-start | bytes 2211848 | tf_op jit(solution)/shard_map/ppermute | solution.py:305
  14.5 35.5 %collective-permute-start.5 = (bf16[1440,256]{1,0:T(8,128)(2,1)S(1)}, bf16[1440,256]{1,0:T(8,128)(2,1)}, u32[]{:S(2)}, u32[]{:S(2)}) collective-permute-start(bf16[1440,256]{1,0:T(8,128)(2,1)S(1)} %maximum_select_fusion.refs_32_), channel_id=1, source_target_pairs={{0,16},{1,17},{2,18},{3,19},{4,20},{5,21},{6,22},{7,23},{8,24},{9,... | collective-permute-start | bytes 2211848 | tf_op jit(solution)/shard_map/ppermute | solution.py:305
  16.1 34.0 %collective-permute-start.6 = (bf16[1440,256]{1,0:T(8,128)(2,1)S(1)}, bf16[1440,256]{1,0:T(8,128)(2,1)}, u32[]{:S(2)}, u32[]{:S(2)}) collective-permute-start(bf16[1440,256]{1,0:T(8,128)(2,1)S(1)} %maximum_select_fusion.refs_32_), channel_id=1, source_target_pairs={{0,2},{1,3},{2,4},{3,5},{4,6},{5,7},{6,0},{7,1},{8,10},{9,11},{10,... | collective-permute-start | bytes 2211848 | tf_op jit(solution)/shard_map/ppermute | solution.py:305
  50.0 31.5 %collective-permute-start.7 = (bf16[1440,256]{1,0:T(8,128)(2,1)}, bf16[1440,256]{1,0:T(8,128)(2,1)S(1)}, u32[]{:S(2)}, u32[]{:S(2)}) collective-permute-start(bf16[1440,256]{1,0:T(8,128)(2,1)} %collective-permute-done.5.refs_34_), channel_id=1, source_target_pairs={{0,8},{1,9},{2,10},{3,11},{4,12},{5,13},{6,14},{7,15},{8,0},{9,1},... | collective-permute-start | bytes 2211848 | tf_op jit(solution)/shard_map/ppermute | solution.py:305
  50.6 30.9 %collective-permute-start.8 = (bf16[1440,256]{1,0:T(8,128)(2,1)}, bf16[1440,256]{1,0:T(8,128)(2,1)S(1)}, u32[]{:S(2)}, u32[]{:S(2)}) collective-permute-start(bf16[1440,256]{1,0:T(8,128)(2,1)} %collective-permute-done.6.refs_36_), channel_id=1, source_target_pairs={{0,16},{1,17},{2,18},{3,19},{4,20},{5,21},{6,22},{7,23},{8,24},{9,... | collective-permute-start | bytes 2211848 | tf_op jit(solution)/shard_map/ppermute | solution.py:305
  51.1 30.4 %collective-permute-start.9 = (bf16[1440,256]{1,0:T(8,128)(2,1)S(1)}, bf16[1440,256]{1,0:T(8,128)(2,1)}, u32[]{:S(2)}, u32[]{:S(2)}) collective-permute-start(bf16[1440,256]{1,0:T(8,128)(2,1)S(1)} %maximum_select_fusion.refs_32_), channel_id=1, source_target_pairs={{0,6},{1,7},{2,0},{3,1},{4,2},{5,3},{6,4},{7,5},{8,14},{9,15},{10,... | collective-permute-start | bytes 2211848 | tf_op jit(solution)/shard_map/ppermute | solution.py:305
  53.2 55.1 %collective-permute-start.10 = (bf16[1440,256]{1,0:T(8,128)(2,1)}, bf16[1440,256]{1,0:T(8,128)(2,1)}, u32[]{:S(2)}, u32[]{:S(2)}) collective-permute-start(bf16[1440,256]{1,0:T(8,128)(2,1)} %collective-permute-done.6.refs_36_), channel_id=1, source_target_pairs={{0,8},{1,9},{2,10},{3,11},{4,12},{5,13},{6,14},{7,15},{8,0},{9,1},... | collective-permute-start | bytes 2211848 | tf_op jit(solution)/shard_map/ppermute | solution.py:305
  54.9 53.4 %collective-permute-start.11 = (bf16[1440,256]{1,0:T(8,128)(2,1)}, bf16[1440,256]{1,0:T(8,128)(2,1)}, u32[]{:S(2)}, u32[]{:S(2)}) collective-permute-start(bf16[1440,256]{1,0:T(8,128)(2,1)} %collective-permute-done.6.refs_36_), channel_id=1, source_target_pairs={{0,2},{1,3},{2,4},{3,5},{4,6},{5,7},{6,0},{7,1},{8,10},{9,11},{10,... | collective-permute-start | bytes 2211848 | tf_op jit(solution)/shard_map/ppermute | solution.py:305
  108.3 27.0 %collective-permute-start.12 = (bf16[1440,256]{1,0:T(8,128)(2,1)}, bf16[1440,256]{1,0:T(8,128)(2,1)S(1)}, u32[]{:S(2)}, u32[]{:S(2)}) collective-permute-start(bf16[1440,256]{1,0:T(8,128)(2,1)} %collective-permute-done.11.refs_44_), channel_id=1, source_target_pairs={{0,8},{1,9},{2,10},{3,11},{4,12},{5,13},{6,14},{7,15},{8,0},{9,1},... | collective-permute-start | bytes 2211848 | tf_op jit(solution)/shard_map/ppermute | solution.py:305
  108.7 60.8 %collective-permute-start.13 = (bf16[512,1024]{1,0:T(8,128)(2,1)}, bf16[512,1024]{1,0:T(8,128)(2,1)S(1)}, u32[]{:S(2)}, u32[]{:S(2)}) collective-permute-start(bf16[512,1024]{1,0:T(8,128)(2,1)} %get-tuple-element.54), channel_id=1, source_target_pairs={{0,1},{1,0},{2,3},{3,2},{4,5},{5,4},{6,7},{7,6},{8,9},{9,8},{10,11... | collective-permute-start | bytes 3145736 | tf_op jit(solution)/shard_map/ppermute | solution.py:305
  136.2 37.1 %collective-permute-start.14 = (bf16[512,1024]{1,0:T(8,128)(2,1)}, bf16[512,1024]{1,0:T(8,128)(2,1)S(1)}, u32[]{:S(2)}, u32[]{:S(2)}) collective-permute-start(bf16[512,1024]{1,0:T(8,128)(2,1)} %get-tuple-element.55), channel_id=1, source_target_pairs={{0,1},{1,0},{2,3},{3,2},{4,5},{5,4},{6,7},{7,6},{8,9},{9,8},{10,11... | collective-permute-start | bytes 3145736 | tf_op jit(solution)/shard_map/ppermute | solution.py:305
  136.7 32.7 %collective-permute-start.18 = (bf16[1440,256]{1,0:T(8,128)(2,1)}, bf16[1440,256]{1,0:T(8,128)(2,1)}, u32[]{:S(2)}, u32[]{:S(2)}) collective-permute-start(bf16[1440,256]{1,0:T(8,128)(2,1)} %collective-permute-done.9.refs_40_), channel_id=1, source_target_pairs={{0,8},{1,9},{2,10},{3,11},{4,12},{5,13},{6,14},{7,15},{8,0},{9,1},... | collective-permute-start | bytes 2211848 | tf_op jit(solution)/shard_map/ppermute | solution.py:305
  153.7 13.7 %collective-permute-start.15 = (bf16[128,1024]{1,0:T(8,128)(2,1)}, bf16[128,1024]{1,0:T(8,128)(2,1)S(1)}, u32[]{:S(2)}, u32[]{:S(2)}) collective-permute-start(bf16[128,1024]{1,0:T(8,128)(2,1)} %get-tuple-element.58), channel_id=1, source_target_pairs={{0,1},{1,0},{2,3},{3,2},{4,5},{5,4},{6,7},{7,6},{8,9},{9,8},{10,11... | collective-permute-start | bytes 786440 | tf_op jit(solution)/shard_map/ppermute | solution.py:305
  166.9 1.9 collective-permute-start.16
  167.4 19.7 %collective-permute-start.21 = (bf16[1440,256]{1,0:T(8,128)(2,1)}, bf16[1440,256]{1,0:T(8,128)(2,1)}, u32[]{:S(2)}, u32[]{:S(2)}) collective-permute-start(bf16[1440,256]{1,0:T(8,128)(2,1)} %collective-permute-done.11.refs_44_), channel_id=1, source_target_pairs={{0,16},{1,17},{2,18},{3,19},{4,20},{5,21},{6,22},{7,23},{8,24},{9,... | collective-permute-start | bytes 2211848 | tf_op jit(solution)/shard_map/ppermute | solution.py:305
  168.8 34.1 %collective-permute-start.19 = (bf16[1440,256]{1,0:T(8,128)(2,1)}, bf16[1440,256]{1,0:T(8,128)(2,1)}, u32[]{:S(2)}, u32[]{:S(2)}) collective-permute-start(bf16[1440,256]{1,0:T(8,128)(2,1)} %collective-permute-done.9.refs_40_), channel_id=1, source_target_pairs={{0,16},{1,17},{2,18},{3,19},{4,20},{5,21},{6,22},{7,23},{8,24},{9,... | collective-permute-start | bytes 2211848 | tf_op jit(solution)/shard_map/ppermute | solution.py:305
  169.5 21.3 %collective-permute-start.17 = (bf16[1440,256]{1,0:T(8,128)(2,1)S(1)}, bf16[1440,256]{1,0:T(8,128)(2,1)}, u32[]{:S(2)}, u32[]{:S(2)}) collective-permute-start(bf16[1440,256]{1,0:T(8,128)(2,1)S(1)} %copy-done.9), channel_id=1, source_target_pairs={{0,2},{1,3},{2,4},{3,5},{4,6},{5,7},{6,0},{7,1},{8,10},{9,11},{10,... | collective-permute-start | bytes 2211848 | tf_op jit(solution)/shard_map/ppermute | solution.py:305
  169.5 34.7 %collective-permute-start.20 = (bf16[1440,256]{1,0:T(8,128)(2,1)S(1)}, bf16[1440,256]{1,0:T(8,128)(2,1)}, u32[]{:S(2)}, u32[]{:S(2)}) collective-permute-start(bf16[1440,256]{1,0:T(8,128)(2,1)S(1)} %copy-done.9), channel_id=1, source_target_pairs={{0,6},{1,7},{2,0},{3,1},{4,2},{5,3},{6,4},{7,5},{8,14},{9,15},{10,... | collective-permute-start | bytes 2211848 | tf_op jit(solution)/shard_map/ppermute | solution.py:305
  173.3 44.5 %collective-permute-start.22 = (bf16[1440,256]{1,0:T(8,128)(2,1)}, bf16[1440,256]{1,0:T(8,128)(2,1)}, u32[]{:S(2)}, u32[]{:S(2)}) collective-permute-start(bf16[1440,256]{1,0:T(8,128)(2,1)} %copy-done.11), channel_id=1, source_target_pairs={{0,16},{1,17},{2,18},{3,19},{4,20},{5,21},{6,22},{7,23},{8,24},{9,... | collective-permute-start | bytes 2211848 | tf_op jit(solution)/shard_map/ppermute | solution.py:305
  235.5 5.7 %collective-permute-start.23 = (bf16[1440,512]{1,0:T(8,128)(2,1)}, bf16[1440,512]{1,0:T(8,128)(2,1)S(1)}, u32[]{:S(2)}, u32[]{:S(2)}) collective-permute-start(bf16[1440,512]{1,0:T(8,128)(2,1)} %get-tuple-element.67), channel_id=1, source_target_pairs={{0,1},{1,0},{2,3},{3,2},{4,5},{5,4},{6,7},{7,6},{8,9},{9,8},{10,11... | collective-permute-start | bytes 4423688 | tf_op jit(solution)/shard_map/ppermute | solution.py:305
  (17 other events, 231.7 us)

commit v3 on v2

v3 whole, which is shorter than its diff:
```python
import functools

import jax
import jax.numpy as jnp
from jax import lax
from jax.experimental import pallas as pl
from jax.experimental.pallas import tpu as pltpu
from jax.sharding import PartitionSpec as P

KVH = 8
HD = 64
BLK = 128
MASKED = -1e30
TRUSTED = 1e26
AXES = ("gx", "gy")
VMEM_LIMIT = 60 * 1024 * 1024


def contract_last(a, b):
    return lax.dot_general(a, b, (((1,), (1,)), ((), ())), preferred_element_type=jnp.float32)


def dot(a, b):
    return jnp.dot(a, b, preferred_element_type=jnp.float32)


def attend_kernel(for_busy, chained, first, at, scal, *refs):
    q_here, bias_here, q_there, bias_there = refs[0:4]
    here, there = refs[4:8], refs[8:12]
    sink_ref = refs[12]
    out_ref, kx_all, vx_all, qx, sums, arrived = refs[13 + chained :]
    step = pl.program_id(1)
    block = step + first
    here_busy = scal[3] > 0
    use_here = here_busy if for_busy else jnp.logical_not(here_busy)
    cache_rows = here[0].shape[0]
    key_rows = kx_all.shape[1]
    tree_rows = key_rows - cache_rows
    groups = q_here.shape[1] // HD // 2
    node_total = jnp.where(use_here, scal[1], scal[4])
    cache_total = jnp.where(use_here, scal[2], scal[5])
    which = pl.program_id(0)
    pairs = kx_all.shape[0]
    kx, vx = kx_all.at[which], vx_all.at[which]
    lane_pair = scal[0] * (KVH // 4) + at + which
    sink_base = lane_pair * (2 * groups)

    def loads(source, pair):
        cols = pl.ds(pl.multiple_of((scal[0] * (KVH // 4) + at + pair) * BLK, BLK), BLK)
        kc_ref, vc_ref, kt_ref, vt_ref = source
        low, high = pl.ds(0, cache_rows), pl.ds(cache_rows, tree_rows)
        lanes, tree = pl.ds(0, BLK), pl.ds(0, tree_rows)
        return (
            pltpu.make_async_copy(kc_ref.at[low, cols], kx_all.at[pair, low, lanes], arrived.at[pair, 0]),
            pltpu.make_async_copy(kt_ref.at[tree, cols], kx_all.at[pair, high, lanes], arrived.at[pair, 1]),
            pltpu.make_async_copy(vc_ref.at[low, cols], vx_all.at[pair, low, lanes], arrived.at[pair, 2]),
            pltpu.make_async_copy(vt_ref.at[tree, cols], vx_all.at[pair, high, lanes], arrived.at[pair, 3]),
        )

    @pl.when((step == 0) & (which == 0))
    def _():
        @pl.when(use_here)
        def _():
            for pair in range(pairs):
                for load in loads(here, pair):
                    load.start()

        @pl.when(jnp.logical_not(use_here))
        def _():
            for pair in range(pairs):
                for load in loads(there, pair):
                    load.start()

        row = lax.broadcasted_iota(jnp.int32, (cache_rows, BLK), 0)
        hidden = jnp.where(row < cache_total, 0.0, MASKED).astype(jnp.bfloat16)
        for pair in range(pairs):
            vx_all[pair, :, BLK : 2 * BLK] = jnp.ones((key_rows, BLK), jnp.bfloat16)
            kx_all[pair, 0:cache_rows, BLK : 2 * BLK] = hidden
        src = lax.broadcasted_iota(jnp.int32, (BLK, BLK), 0)
        dst = lax.broadcasted_iota(jnp.int32, (BLK, BLK), 1)
        own = jnp.where(src == dst, 1.0, 0.0).astype(jnp.bfloat16)
        for head in (0, 1):
            for g in range(groups):
                qx[head, g * BLK : (g + 1) * BLK, BLK : 2 * BLK] = own

    live = block * BLK < node_total
    lane = lax.broadcasted_iota(jnp.int32, (BLK, BLK), 1)
    low = lane < HD
    zero = jnp.zeros((BLK, BLK), jnp.float32)

    @pl.when(live)
    def _():
        kx[cache_rows:key_rows, BLK : 2 * BLK] = jnp.where(use_here, bias_here[...], bias_there[...])
        for head in (0, 1):
            for pair in range(groups // 2):
                cols = slice((head * groups // 2 + pair) * BLK, (head * groups // 2 + pair + 1) * BLK)
                both = jnp.where(use_here, q_here[:, cols], q_there[:, cols]).astype(jnp.float32) * (HD**-0.5)
                turned = pltpu.roll(both, HD, 1)
                if head == 0:
                    upper, lower = jnp.where(low, both, zero), jnp.where(low, turned, zero)
                else:
                    upper, lower = jnp.where(low, zero, turned), jnp.where(low, zero, both)
                at_row = 2 * pair * BLK
                qx[head, at_row : at_row + BLK, 0:BLK] = upper.astype(jnp.bfloat16)
                qx[head, at_row + BLK : at_row + 2 * BLK, 0:BLK] = lower.astype(jnp.bfloat16)

    @pl.when(step == 0)
    def _():
        for load in loads(here, which):
            load.wait()

    @pl.when(live)
    def _():
        node = lax.broadcasted_iota(jnp.int32, (BLK, BLK), 0) + block * BLK

        def finish(with_sink):
            worst = zero
            for head in (0, 1):
                for pair in range(groups // 2):
                    parts = []
                    for g in (2 * pair, 2 * pair + 1):
                        rows = slice(g * BLK, (g + 1) * BLK)
                        under = sums[head, rows, BLK : 2 * BLK]
                        if with_sink:
                            under = under + sink_ref[1, sink_base + head * groups + g]
                        worst = jnp.maximum(worst, under)
                        parts.append(sums[head, rows, 0:BLK] / under)
                    if head == 0:
                        joined = jnp.where(low, parts[0], pltpu.roll(parts[1], HD, 1))
                    else:
                        joined = jnp.where(low, pltpu.roll(parts[0], HD, 1), parts[1])
                    cols = slice((head * groups // 2 + pair) * BLK, (head * groups // 2 + pair + 1) * BLK)
                    out_ref[:, cols] = jnp.where(node < node_total, joined, zero).astype(jnp.bfloat16)
            return worst

        def quick(head, carry):
            weights = jnp.exp(contract_last(qx[head], kx[...])).astype(jnp.bfloat16)
            sums[head] = dot(weights, vx[...])
            return carry

        lax.fori_loop(0, 2, quick, 0)
        worst = finish(True)

        @pl.when(jnp.logical_not(jnp.max(worst) < TRUSTED))
        def _():
            def careful(g, carry):
                for head in (0, 1):
                    rows = pl.ds(pl.multiple_of(g * BLK, BLK), BLK)
                    scores = contract_last(qx[head, rows, :], kx[...])
                    sink = sink_ref[0, sink_base + head * groups + g]
                    peak = jnp.maximum(jnp.max(scores, axis=1, keepdims=True), sink)
                    weights = jnp.exp(scores - peak).astype(jnp.bfloat16)
                    part = dot(weights, vx[...])
                    sums[head, rows, 0:BLK] = part[:, 0:BLK]
                    sums[head, rows, BLK : 2 * BLK] = part[:, BLK : 2 * BLK] + jnp.exp(sink - peak)
                return carry

            lax.fori_loop(0, groups, careful, 0)
            finish(False)

    @pl.when(jnp.logical_not(live))
    def _():
        out_ref[...] = jnp.zeros_like(out_ref)


def attend(scal, here, there, sinks, for_busy, at, pairs, first, count, rows, tree_rows, before):
    q, *kv, bias = here
    q_got, *kv_got, bias_got = there
    cache_rows = kv[0].shape[0]
    width = q.shape[1] // (KVH // 2)
    keys = cache_rows + tree_rows
    per_core = KVH // 4
    anywhere = pl.BlockSpec(memory_space=pl.ANY)
    in_specs = [
        pl.BlockSpec((BLK, width), lambda p, i, s: (first + i, s[0] * per_core + at + p)),
        pl.BlockSpec((tree_rows, BLK), lambda p, i, s: (0, first + i)),
        pl.BlockSpec((BLK, width), lambda p, i, s: (first + i, at + p)),
        pl.BlockSpec((tree_rows, BLK), lambda p, i, s: (0, first + i)),
        *[anywhere] * 8,
        pl.BlockSpec(memory_space=pltpu.SMEM),
    ]
    operands = [q, bias, q_got, bias_got, *kv, *kv_got, sinks]
    aliases = {}
    if before is not None:
        aliases[1 + len(operands)] = 0
        in_specs.append(anywhere)
        operands.append(before)
    groups = width // HD // 2
    work = pairs * count * BLK * 2 * groups * keys
    return pl.pallas_call(
        functools.partial(attend_kernel, for_busy, len(aliases), first, at),
        grid_spec=pltpu.PrefetchScalarGridSpec(
            num_scalar_prefetch=1,
            grid=(pairs, count),
            in_specs=in_specs,
            out_specs=pl.BlockSpec((BLK, width), lambda p, i, s: (first + i, p)),
            scratch_shapes=[
                pltpu.VMEM((pairs, keys, 2 * BLK), jnp.bfloat16),
                pltpu.VMEM((pairs, keys, 2 * BLK), jnp.bfloat16),
                pltpu.VMEM((2, groups * BLK, 2 * BLK), jnp.bfloat16),
                pltpu.VMEM((2, groups * BLK, 2 * BLK), jnp.float32),
                pltpu.SemaphoreType.DMA((pairs, 4)),
            ],
        ),
        out_shape=jax.ShapeDtypeStruct((rows, pairs * width), jnp.bfloat16),
        input_output_aliases=aliases,
        compiler_params=pltpu.CompilerParams(vmem_limit_bytes=VMEM_LIMIT),
        cost_estimate=pl.CostEstimate(
            flops=work * 2 * 4 * BLK, bytes_accessed=8 * keys * BLK, transcendentals=work
        ),
        name="attend",
    )(scal, *operands)


def tree_bias(words_t, key_total):
    spread = jnp.repeat(words_t, 32, axis=0)
    shift = (jnp.arange(key_total, dtype=jnp.int32) % 32)[:, None]
    flag = jnp.bitwise_and(lax.shift_right_logical(spread, jnp.broadcast_to(shift, spread.shape)), 1)
    return jnp.where(flag > 0, 0.0, MASKED).astype(jnp.bfloat16)


TILES = 6


def project_kernel(blocks, info, *refs):
    busy_mine, busy_got, light_mine, light_got = refs[0:2], refs[2:4], refs[4], refs[5]
    weights = refs[6 : 6 + blocks]
    own_ref, other_ref, attended, x, w, blank, came, left = refs[6 + blocks :]
    step = pl.program_id(0)
    nodes, width = busy_mine[0].shape
    few = light_mine.shape[0]
    depth = weights[0].shape[1]
    here_busy = info[0] > 0

    def loads(core, mine):
        busy, light = (busy_mine, light_mine) if mine else (busy_got, light_got)
        base = core * 2 * width
        for m in (0, 1):
            yield pltpu.make_async_copy(
                busy[m], x.at[pl.ds(0, nodes), pl.ds(base + m * width, width)], came.at[core, m]
            )
        yield pltpu.make_async_copy(light, x.at[pl.ds(nodes, few), pl.ds(base, 2 * width)], came.at[core, 2])

    def busy_stores():
        return [pltpu.make_async_copy(x.at[pl.ds(0, nodes), :], attended, left.at[0])]

    def light_stores():
        return [
            pltpu.make_async_copy(x.at[pl.ds(nodes, few), :], attended.at[pl.ds(0, few), :], left.at[0]),
            pltpu.make_async_copy(blank, attended.at[pl.ds(few, nodes - few), :], left.at[1]),
        ]

    def for_either(act):
        @pl.when(here_busy)
        def _():
            for copy in busy_stores():
                act(copy)

        @pl.when(jnp.logical_not(here_busy))
        def _():
            for copy in light_stores():
                act(copy)

    @pl.when(step == 0)
    def _():
        for core in (0, 1):
            for mine in (True, False):

                @pl.when((info[1] == core) == mine)
                def _():
                    for copy in loads(core, mine):
                        copy.start()

        blank[...] = jnp.zeros_like(blank)

    for k in range(blocks):
        w[:, pl.ds(pl.multiple_of(info[2 + k] * depth, depth), depth)] = weights[k][...]

    @pl.when(step == 0)
    def _():
        for core in (0, 1):
            for copy in loads(core, True):
                copy.wait()
        for_either(lambda copy: copy.start())

    done = contract_last(w[...], x[...]).astype(jnp.bfloat16)
    rest = jnp.zeros((done.shape[0], nodes - few), jnp.bfloat16)

    @pl.when(here_busy)
    def _():
        own_ref[...] = done[:, :nodes]
        other_ref[:, 0:few] = done[:, nodes:]
        other_ref[:, few:] = rest

    @pl.when(jnp.logical_not(here_busy))
    def _():
        other_ref[...] = done[:, :nodes]
        own_ref[:, 0:few] = done[:, nodes:]
        own_ref[:, few:] = rest

    @pl.when(step == pl.num_programs(0) - 1)
    def _():
        for_either(lambda copy: copy.wait())


def project(info, pieces, blocks):
    columns, depth = blocks[0].shape
    tile = columns // TILES
    nodes, few = pieces[0].shape[0], pieces[4].shape[0]
    total = depth * len(blocks)
    anywhere = pl.BlockSpec(memory_space=pl.ANY)
    return pl.pallas_call(
        functools.partial(project_kernel, len(blocks)),
        grid_spec=pltpu.PrefetchScalarGridSpec(
            num_scalar_prefetch=1,
            grid=(TILES,),
            in_specs=[anywhere] * len(pieces)
            + [pl.BlockSpec((tile, depth), lambda i, s: (i, 0))] * len(blocks),
            out_specs=[
                pl.BlockSpec((tile, nodes), lambda i, s: (s[1] * TILES + i, 0)),
                pl.BlockSpec((tile, nodes), lambda i, s: (i, 0)),
                anywhere,
            ],
            scratch_shapes=[
                pltpu.VMEM((nodes + few, total), jnp.bfloat16),
                pltpu.VMEM((tile, total), jnp.bfloat16),
                pltpu.VMEM((nodes - few, total), jnp.bfloat16),
                pltpu.SemaphoreType.DMA((2, 3)),
                pltpu.SemaphoreType.DMA((2,)),
            ],
        ),
        out_shape=[
            jax.ShapeDtypeStruct((2 * columns, nodes), jnp.bfloat16),
            jax.ShapeDtypeStruct((columns, nodes), jnp.bfloat16),
            jax.ShapeDtypeStruct((nodes, total), jnp.bfloat16),
        ],
        compiler_params=pltpu.CompilerParams(vmem_limit_bytes=VMEM_LIMIT),
        cost_estimate=pl.CostEstimate(
            flops=2 * (nodes + few) * columns * total, bytes_accessed=2 * columns * total, transcendentals=0
        ),
        name="project",
    )(info, *pieces, *blocks)


def on_device(plane, line, args):
    (
        q_nodes, k_cache, v_cache, k_tree, v_tree, anc_bits, node_count, cache_len, sinks, o_weight,
    ) = args
    gx = lax.axis_index("gx")
    gy = lax.axis_index("gy")
    core = gy % 2
    far = 1 - core
    z = gy // 2
    is_busy = (gx + gy) % 2 == 0
    places = [(a, b, c) for a in range(plane) for b in range(line) for c in range(2)]

    def number(a, b, c):
        return (a * line + b) * 2 + c

    def moved(x, to):
        pairs = [(number(*p), number(*to(*p))) for p in places]
        return lax.ppermute(x, AXES, pairs)

    def swapped(x):
        return moved(x, lambda a, b, c: (a, b, 1 - c))

    q, kc, vc, kt, vt = q_nodes[0], k_cache[0], v_cache[0], k_tree[0], v_tree[0]
    node_total = q.shape[0]
    tree_rows = kt.shape[0]
    columns = o_weight.shape[1] // 2
    half_q = q.shape[1] // 2

    w_t = o_weight.T
    w_mine = lax.dynamic_slice_in_dim(w_t, core * columns, columns, 0)
    w_theirs = swapped(lax.dynamic_slice_in_dim(w_t, far * columns, columns, 0))
    b0 = jnp.where(
        core == 0,
        jnp.concatenate([w_mine, w_theirs], axis=1),
        jnp.concatenate([w_theirs, w_mine], axis=1),
    )

    words_t = anc_bits[0].T
    words = words_t.shape[0]
    spot = jnp.arange(words + 2, dtype=jnp.int32)[:, None]
    note = jnp.pad(words_t, ((0, 2), (0, 0)))
    note = jnp.where(spot == words, node_count[0], jnp.where(spot == words + 1, cache_len[0], note))
    kv = (kc, vc, kt, vt)
    kv_got = tuple(swapped(a) for a in kv)
    q_got = swapped(lax.dynamic_slice_in_dim(q, far * half_q, half_q, 1))
    note_got = swapped(note)
    here = (q, *kv, tree_bias(words_t, tree_rows))
    there = (q_got, *kv_got, tree_bias(note_got[:words], tree_rows))

    def table(values):
        spot = jnp.arange(len(values), dtype=jnp.int32)
        out = jnp.zeros((len(values),), jnp.int32)
        for i, v in enumerate(values):
            out = jnp.where(spot == i, v, out)
        return out

    flags = table(
        [core, node_count[0], cache_len[0], is_busy.astype(jnp.int32), note_got[words, 0], note_got[words + 1, 0]]
    )
    sink_table = jnp.stack([sinks, jnp.exp(sinks)])
    half = node_total // BLK // 2

    def attend_busy(at, first, before):
        return attend(
            flags, here, there, sink_table, True, at, 1, first, half, node_total, tree_rows, before
        )

    def attend_light():
        return attend(flags, here, there, sink_table, False, 0, KVH // 4, 0, 1, BLK, BLK, None)

    direct = plane == 4 and line == 4

    def along_x(x):
        return moved(x, lambda a, b, c: (a ^ 1, b, c))

    def along_y(x):
        return moved(x, lambda a, b, c: (a ^ 2, b, c))

    def along_z(x, by):
        return moved(x, lambda a, b, c: (a, (b + by) % line, c))

    def together(*arrays):
        return lax.optimization_barrier(arrays) if direct else arrays

    if direct:
        x0, y0, z1 = along_x(b0), along_y(b0), along_z(b0, 1)
    else:
        x0 = y0 = z1 = b0
    busy0 = attend_busy(0, 0, None)
    busy0, b0, x0, y0, z1 = together(busy0, b0, x0, y0, z1)
    if direct:
        d0, y1, z3, x1 = along_x(y0), along_y(z1), along_z(b0, 3), along_x(z1)
    else:
        d0 = y1 = z3 = x1 = b0
    busy0 = attend_busy(0, half, busy0)
    busy0, d0, y1, z3, z1 = together(busy0, d0, y1, z3, z1)
    if direct:
        z2, y3 = along_z(z1, 1), along_y(z3)
    else:
        z2 = y3 = b0
    busy1 = attend_busy(1, 0, None)
    busy1, x1, z2, z3, d0 = together(busy1, x1, z2, z3, d0)
    if direct:
        x2, y2, x3 = along_x(z2), along_y(z2), along_x(z3)
        d1, d3 = along_z(d0, 1), along_z(d0, 3)
    else:
        x2 = y2 = x3 = d1 = d3 = b0
    busy1 = attend_busy(1, half, busy1)
    busy1, x2 = together(busy1, x2)
    d2 = along_y(x2) if direct else b0
    light = attend_light()
    got0, got1, light_got = swapped(busy0), swapped(busy1), swapped(light)

    if direct:
        slots = {}
        info = [is_busy.astype(jnp.int32), core]
        for dz in (0, 1, 3, 2):
            for flip in (0, 1, 2, 3):
                slots[(dz, flip)] = len(info)
                info.append((gx ^ flip) * line + (z - dz) % line)
        info = table(info)
        blocks = [
            (b0, (0, 0)), (x0, (0, 1)), (y0, (0, 2)), (d0, (0, 3)),
            (z1, (1, 0)), (x1, (1, 1)), (y1, (1, 2)), (d1, (1, 3)),
            (z3, (3, 0)), (x3, (3, 1)), (y3, (3, 2)), (d3, (3, 3)),
            (z2, (2, 0)), (x2, (2, 1)), (y2, (2, 2)), (d2, (2, 3)),
        ]
        order = sorted(blocks, key=lambda b: slots[b[1]])
        full, other_half, attended = project(info, (busy0, busy1, got0, got1, light, light_got), [b for b, _ in order])
        full = lax.dynamic_update_slice(full, swapped(other_half), (far * columns, 0))
        projected = full.T
    else:

        def in_order(mine, got):
            return jnp.where(
                core == 0, jnp.concatenate([*mine, *got], axis=1), jnp.concatenate([*got, *mine], axis=1)
            )

        padded = jnp.pad(in_order([light], [light_got]), ((0, node_total - BLK), (0, 0)))
        attended = jnp.where(is_busy, in_order([busy0, busy1], [got0, got1]), padded)
        w_all = lax.all_gather(o_weight, AXES, axis=0, tiled=True)
        projected = dot(attended, w_all).astype(jnp.bfloat16)
    return attended[None], projected[None]


def solution(mesh):
    plane, line = mesh.shape["gx"], mesh.shape["gy"] // 2
    rows = P(AXES, None, None)
    placed = (rows, rows, rows, rows, rows, rows, P(AXES), P(AXES), P(), P(AXES, None))

    def run(*args):
        return on_device(plane, line, args)

    return jax.shard_map(run, mesh=mesh, in_specs=placed, out_specs=(rows, rows), check_vma=False)
```

time: 243 us -> 260 us (1.070)
  the two profiles are of different devices: /device:TPU:0 before, /device:TPU:9 now
where the time goes in v3:
time: 260 us; the launch traced here: 258 us
  Pallas kernels  157 us (60%)
  starting transfers between devices  49.4 us (19%)
  waiting for transfers between devices  38.7 us (15%)
  other arithmetic  5.66 us (2%)
  local copies, waits for them, and re-layouts  4.65 us (2%)
    pallas_call x5, Pallas kernels, attend(): pl.pallas_call(functools.partial(attend_kernel, for_busy, len(aliases), f...  138 us
    ppermute x26, starting transfers between devices, moved(): return lax.ppermute(x, AXES, pairs)  49.4 us
    ppermute x26, waiting for transfers between devices, moved(): return lax.ppermute(x, AXES, pairs)  38.7 us
    pallas_call x1, Pallas kernels, project(): pl.pallas_call(functools.partial(project_kernel, len(blocks)), grid_spec=...  18.6 us
  transfers between devices with their start and end apart: 26, of which 4 were waited for; matrix products, arithmetic and copies ran while one was open for 2% of the time, Pallas kernels for 54%

profile of v3, /device:TPU:9, one launch (start us, length us, event | category | flops | bytes accessed | tf_op | source)
XLA Modules:
  0.0 257.5 jit_solution(7867528144435218575)
XLA Ops:
  0.7 1.8 dynamic-slice_bitcast_fusion
  5.8 4.9 %collective-permute-done = s32[18,512]{1,0:T(8,128)S(1)} collective-permute-done((s32[18,512]{1,0:T(8,128)S(1)}, s32[18,512]{1,0:T(8,128)S(1)}, u32[]{:S(2)}, u32[]{:S(2)}) %collective-permute-start) | collective-permute-done | bytes 36896 | tf_op jit(solution)/shard_map/ppermute | solution.py:362
  11.8 1.3 maximum_select_fusion.refs_6_
  13.2 1.3 collective-permute-start.9
  14.5 1.2 collective-permute-start.8
  15.7 1.2 collective-permute-start.7
  17.5 1.3 select_convert_fusion
  18.9 1.7 compare_select_fusion.5.scal
  20.6 34.7 %attend.5.refs_13_ = bf16[512,1024]{1,0:T(8,128)(2,1)} custom-call(s32[6]{0:T(128)} %compare_select_fusion.5.scal, bf16[512,4096]{1,0:T(8,128)(2,1)} %bitcast.45, bf16[512,512]{1,0:T(8,128)(2,1)} %get-tuple-element.47.refs_1_, bf16[512,2048]{1,0:T(8,128)(2,1)} %collective-permute-done.1.refs_2_, bf16[512,512]{1,0:T(8,128)(2,1)} %get-tuple-element.46.refs_3_, ...), custom_call_target="tpu_custom_call" | custom-call | flops 6442450944 | bytes 1572864 | tf_op jit(solution)/shard_map/attend/pallas_call | solution.py:190
  56.0 1.2 collective-permute-start.13
  57.2 19.2 %attend.6.refs_0_ = bf16[512,1024]{1,0:T(8,128)(2,1)} custom-call(s32[6]{0:T(128)} %compare_select_fusion.5.scal, bf16[512,4096]{1,0:T(8,128)(2,1)} %bitcast.46, bf16[512,512]{1,0:T(8,128)(2,1)} %get-tuple-element.47.refs_1_, bf16[512,2048]{1,0:T(8,128)(2,1)} %collective-permute-done.1.refs_2_, ...), custom_call_target="tpu_custom_call", output_to_operand_aliasing={{}: (14, {})} | custom-call | flops 6442450944 | bytes 1572864 | tf_op jit(solution)/shard_map/attend/pallas_call | solution.py:190
  76.5 1.5 collective-permute-start.14
  78.0 34.6 %attend.7.refs_13_ = bf16[512,1024]{1,0:T(8,128)(2,1)} custom-call(s32[6]{0:T(128)} %compare_select_fusion.5.scal, bf16[512,4096]{1,0:T(8,128)(2,1)} %bitcast.47, bf16[512,512]{1,0:T(8,128)(2,1)} %get-tuple-element.47.refs_1_, bf16[512,2048]{1,0:T(8,128)(2,1)} %collective-permute-done.1.refs_2_, bf16[512,512]{1,0:T(8,128)(2,1)} %get-tuple-element.46.refs_3_, ...), custom_call_target="tpu_custom_call" | custom-call | flops 6442450944 | bytes 1572864 | tf_op jit(solution)/shard_map/attend/pallas_call | solution.py:190
  112.7 2.7 %collective-permute-start.16 = (bf16[512,1024]{1,0:T(8,128)(2,1)}, bf16[512,1024]{1,0:T(8,128)(2,1)S(1)}, u32[]{:S(2)}, u32[]{:S(2)}) collective-permute-start(bf16[512,1024]{1,0:T(8,128)(2,1)} %attend.6.refs_0_), channel_id=1, source_target_pairs={{0,1},{1,0},{2,3},{3,2},{4,5},{5,4},{6,7},{7,6},{8,9},{9,8},{10,11... | collective-permute-start | bytes 3145736 | tf_op jit(solution)/shard_map/ppermute | solution.py:362
  115.3 15.1 %collective-permute-start.15 = (bf16[1440,256]{1,0:T(8,128)(2,1)}, bf16[1440,256]{1,0:T(8,128)(2,1)}, u32[]{:S(2)}, u32[]{:S(2)}) collective-permute-start(bf16[1440,256]{1,0:T(8,128)(2,1)} %collective-permute-done.14.refs_18_), channel_id=1, source_target_pairs={{0,8},{1,9},{2,10},{3,11},{4,12},{5,13},{6,14},{7,15},{8,0},{9,1},... | collective-permute-start | bytes 2211848 | tf_op jit(solution)/shard_map/ppermute | solution.py:362
  130.4 30.6 %attend.9.refs_4_ = bf16[128,2048]{1,0:T(8,128)(2,1)} custom-call(s32[6]{0:T(128)} %compare_select_fusion.5.scal, bf16[512,4096]{1,0:T(8,128)(2,1)} %bitcast.48, bf16[512,512]{1,0:T(8,128)(2,1)} %get-tuple-element.47.refs_1_, bf16[512,2048]{1,0:T(8,128)(2,1)} %collective-permute-done.1.refs_2_, bf16[512,512]{1,0:T(8,128)(2,1)} %get-tuple-element.46.refs_3_, ...), custom_call_target="tpu_custom_call" | custom-call | flops 4831838208 | bytes 1179648 | tf_op jit(solution)/shard_map/attend/pallas_call | solution.py:190
  161.5 2.0 collective-permute-start.21
  163.4 19.2 %attend.8.refs_1_ = bf16[512,1024]{1,0:T(8,128)(2,1)} custom-call(s32[6]{0:T(128)} %compare_select_fusion.5.scal, bf16[512,4096]{1,0:T(8,128)(2,1)} %bitcast.49, bf16[512,512]{1,0:T(8,128)(2,1)} %get-tuple-element.47.refs_1_, bf16[512,2048]{1,0:T(8,128)(2,1)} %collective-permute-done.1.refs_2_, ...), custom_call_target="tpu_custom_call", output_to_operand_aliasing={{}: (14, {})} | custom-call | flops 6442450944 | bytes 1572864 | tf_op jit(solution)/shard_map/attend/pallas_call | solution.py:190
  183.5 16.6 %collective-permute-start.22 = (bf16[1440,256]{1,0:T(8,128)(2,1)S(1)}, bf16[1440,256]{1,0:T(8,128)(2,1)}, u32[]{:S(2)}, u32[]{:S(2)}) collective-permute-start(bf16[1440,256]{1,0:T(8,128)(2,1)S(1)} %copy-done.7), channel_id=1, source_target_pairs={{0,6},{1,7},{2,0},{3,1},{4,2},{5,3},{6,4},{7,5},{8,14},{9,15},{10,... | collective-permute-start | bytes 2211848 | tf_op jit(solution)/shard_map/ppermute | solution.py:362
  200.2 1.5 collective-permute-start.24
  202.2 29.5 %collective-permute-done.22.refs_17_ = bf16[1440,256]{1,0:T(8,128)(2,1)} collective-permute-done((bf16[1440,256]{1,0:T(8,128)(2,1)S(1)}, bf16[1440,256]{1,0:T(8,128)(2,1)}, u32[]{:S(2)}, u32[]{:S(2)}) %collective-permute-start.22) | collective-permute-done | bytes 737312 | tf_op jit(solution)/shard_map/ppermute | solution.py:362
  233.9 18.6 %project.1 = (bf16[2880,512]{1,0:T(8,128)(2,1)}, bf16[1440,512]{1,0:T(8,128)(2,1)}, bf16[512,4096]{1,0:T(8,128)(2,1)}) custom-call(s32[18]{0:T(128)} %fusion.8.info, bf16[512,1024]{1,0:T(8,128)(2,1)} %attend.6.refs_0_, bf16[512,1024]{1,0:T(8,128)(2,1)} %attend.8.refs_1_, bf16[512,1024]{1,0:T(8,128)(2,1)} %copy-done.4, bf16[512,1024]{1,0:T(8,128)(2,1)} %copy-done.5, ...), custom_call_target="tpu_custom_call" | custom-call | flops 7549747200 | bytes 11796480 | tf_op jit(solution)/shard_map/project/pallas_call | solution.py:312
  253.2 3.1 %collective-permute-done.25 = bf16[1440,512]{1,0:T(8,128)(2,1)S(1)} collective-permute-done((bf16[1440,512]{1,0:T(8,128)(2,1)}, bf16[1440,512]{1,0:T(8,128)(2,1)S(1)}, u32[]{:S(2)}, u32[]{:S(2)}) %collective-permute-start.25) | collective-permute-done | bytes 1474592 | tf_op jit(solution)/shard_map/ppermute | solution.py:362
  256.3 1.2 constant_dynamic-update-slice_fusion
  (70 shorter events, 9.2 us)
Async XLA Ops:
  2.5 18.1 %collective-permute-start.1 = (bf16[512,2048]{1,0:T(8,128)(2,1)S(1)}, bf16[512,2048]{1,0:T(8,128)(2,1)}, u32[]{:S(2)}, u32[]{:S(2)}) collective-permute-start(bf16[512,2048]{1,0:T(8,128)(2,1)S(1)} %dynamic-slice_bitcast_fusion), channel_id=1, source_target_pairs={{0,1},{1,0},{2,3},{3,2},{4,5},{5,4},{6,7},{7,6},{8,9},{9,8},{10,11... | collective-permute-start | bytes 6291464 | tf_op jit(solution)/shard_map/ppermute | solution.py:362
  3.3 7.8 %collective-permute-start.6 = (bf16[1440,128]{1,0:T(8,128)(2,1)S(1)}, bf16[1440,128]{1,0:T(8,128)(2,1)}, u32[]{:S(2)}, u32[]{:S(2)}) collective-permute-start(bf16[1440,128]{1,0:T(8,128)(2,1)S(1)} %get-tuple-element.43), channel_id=1, source_target_pairs={{0,1},{1,0},{2,3},{3,2},{4,5},{5,4},{6,7},{7,6},{8,9},{9,8},{10,11... | collective-permute-start | bytes 1105928 | tf_op jit(solution)/shard_map/ppermute | solution.py:362
  3.4 12.4 %collective-permute-start.2 = (bf16[1024,512]{1,0:T(8,128)(2,1)}, bf16[1024,512]{1,0:T(8,128)(2,1)}, u32[]{:S(2)}, u32[]{:S(2)}) collective-permute-start(bf16[1024,512]{1,0:T(8,128)(2,1)} %bitcast.54), channel_id=1, source_target_pairs={{0,1},{1,0},{2,3},{3,2},{4,5},{5,4},{6,7},{7,6},{8,9},{9,8},{10,11... | collective-permute-start | bytes 3145736 | tf_op jit(solution)/shard_map/ppermute | solution.py:362
  3.9 16.8 %collective-permute-start.3 = (bf16[1024,512]{1,0:T(8,128)(2,1)}, bf16[1024,512]{1,0:T(8,128)(2,1)}, u32[]{:S(2)}, u32[]{:S(2)}) collective-permute-start(bf16[1024,512]{1,0:T(8,128)(2,1)} %bitcast.60), channel_id=1, source_target_pairs={{0,1},{1,0},{2,3},{3,2},{4,5},{5,4},{6,7},{7,6},{8,9},{9,8},{10,11... | collective-permute-start | bytes 3145736 | tf_op jit(solution)/shard_map/ppermute | solution.py:362
  5.3 5.3 %collective-permute-start = (s32[18,512]{1,0:T(8,128)S(1)}, s32[18,512]{1,0:T(8,128)S(1)}, u32[]{:S(2)}, u32[]{:S(2)}) collective-permute-start(s32[18,512]{1,0:T(8,128)S(1)} %select_select_fusion), channel_id=1, source_target_pairs={{0,1},{1,0},{2,3},{3,2},{4,5},{5,4},{6,7},{7,6},{8,9},{9,8},{10,11... | collective-permute-start | bytes 110600 | tf_op jit(solution)/shard_map/ppermute | solution.py:362
  13.2 42.1 %collective-permute-start.9 = (bf16[1440,256]{1,0:T(8,128)(2,1)S(1)}, bf16[1440,256]{1,0:T(8,128)(2,1)}, u32[]{:S(2)}, u32[]{:S(2)}) collective-permute-start(bf16[1440,256]{1,0:T(8,128)(2,1)S(1)} %maximum_select_fusion.refs_6_), channel_id=1, source_target_pairs={{0,2},{1,3},{2,4},{3,5},{4,6},{5,7},{6,0},{7,1},{8,10},{9,11},{10,... | collective-permute-start | bytes 2211848 | tf_op jit(solution)/shard_map/ppermute | solution.py:362
  14.5 40.8 %collective-permute-start.8 = (bf16[1440,256]{1,0:T(8,128)(2,1)S(1)}, bf16[1440,256]{1,0:T(8,128)(2,1)}, u32[]{:S(2)}, u32[]{:S(2)}) collective-permute-start(bf16[1440,256]{1,0:T(8,128)(2,1)S(1)} %maximum_select_fusion.refs_6_), channel_id=1, source_target_pairs={{0,16},{1,17},{2,18},{3,19},{4,20},{5,21},{6,22},{7,23},{8,24},{9,... | collective-permute-start | bytes 2211848 | tf_op jit(solution)/shard_map/ppermute | solution.py:362
  15.7 39.5 %collective-permute-start.7 = (bf16[1440,256]{1,0:T(8,128)(2,1)S(1)}, bf16[1440,256]{1,0:T(8,128)(2,1)}, u32[]{:S(2)}, u32[]{:S(2)}) collective-permute-start(bf16[1440,256]{1,0:T(8,128)(2,1)S(1)} %maximum_select_fusion.refs_6_), channel_id=1, source_target_pairs={{0,8},{1,9},{2,10},{3,11},{4,12},{5,13},{6,14},{7,15},{8,0},{9,1},... | collective-permute-start | bytes 2211848 | tf_op jit(solution)/shard_map/ppermute | solution.py:362
  55.3 21.1 %collective-permute-start.10 = (bf16[1440,256]{1,0:T(8,128)(2,1)}, bf16[1440,256]{1,0:T(8,128)(2,1)S(1)}, u32[]{:S(2)}, u32[]{:S(2)}) collective-permute-start(bf16[1440,256]{1,0:T(8,128)(2,1)} %collective-permute-done.8.refs_8_), channel_id=1, source_target_pairs={{0,8},{1,9},{2,10},{3,11},{4,12},{5,13},{6,14},{7,15},{8,0},{9,1},... | collective-permute-start | bytes 2211848 | tf_op jit(solution)/shard_map/ppermute | solution.py:362
  55.6 20.8 %collective-permute-start.12 = (bf16[1440,256]{1,0:T(8,128)(2,1)S(1)}, bf16[1440,256]{1,0:T(8,128)(2,1)}, u32[]{:S(2)}, u32[]{:S(2)}) collective-permute-start(bf16[1440,256]{1,0:T(8,128)(2,1)S(1)} %maximum_select_fusion.refs_6_), channel_id=1, source_target_pairs={{0,6},{1,7},{2,0},{3,1},{4,2},{5,3},{6,4},{7,5},{8,14},{9,15},{10,... | collective-permute-start | bytes 2211848 | tf_op jit(solution)/shard_map/ppermute | solution.py:362
  55.8 20.7 %collective-permute-start.11 = (bf16[1440,256]{1,0:T(8,128)(2,1)}, bf16[1440,256]{1,0:T(8,128)(2,1)S(1)}, u32[]{:S(2)}, u32[]{:S(2)}) collective-permute-start(bf16[1440,256]{1,0:T(8,128)(2,1)} %collective-permute-done.9.refs_10_), channel_id=1, source_target_pairs={{0,16},{1,17},{2,18},{3,19},{4,20},{5,21},{6,22},{7,23},{8,24},{9,... | collective-permute-start | bytes 2211848 | tf_op jit(solution)/shard_map/ppermute | solution.py:362
  56.0 59.3 %collective-permute-start.13 = (bf16[1440,256]{1,0:T(8,128)(2,1)}, bf16[1440,256]{1,0:T(8,128)(2,1)S(1)}, u32[]{:S(2)}, u32[]{:S(2)}) collective-permute-start(bf16[1440,256]{1,0:T(8,128)(2,1)} %collective-permute-done.9.refs_10_), channel_id=1, source_target_pairs={{0,8},{1,9},{2,10},{3,11},{4,12},{5,13},{6,14},{7,15},{8,0},{9,1},... | collective-permute-start | bytes 2211848 | tf_op jit(solution)/shard_map/ppermute | solution.py:362
  76.5 38.9 %collective-permute-start.14 = (bf16[1440,256]{1,0:T(8,128)(2,1)}, bf16[1440,256]{1,0:T(8,128)(2,1)}, u32[]{:S(2)}, u32[]{:S(2)}) collective-permute-start(bf16[1440,256]{1,0:T(8,128)(2,1)} %collective-permute-done.9.refs_10_), channel_id=1, source_target_pairs={{0,2},{1,3},{2,4},{3,5},{4,6},{5,7},{6,0},{7,1},{8,10},{9,11},{10,... | collective-permute-start | bytes 2211848 | tf_op jit(solution)/shard_map/ppermute | solution.py:362
  112.7 87.5 %collective-permute-start.16 = (bf16[512,1024]{1,0:T(8,128)(2,1)}, bf16[512,1024]{1,0:T(8,128)(2,1)S(1)}, u32[]{:S(2)}, u32[]{:S(2)}) collective-permute-start(bf16[512,1024]{1,0:T(8,128)(2,1)} %attend.6.refs_0_), channel_id=1, source_target_pairs={{0,1},{1,0},{2,3},{3,2},{4,5},{5,4},{6,7},{7,6},{8,9},{9,8},{10,11... | collective-permute-start | bytes 3145736 | tf_op jit(solution)/shard_map/ppermute | solution.py:362
  115.3 67.3 %collective-permute-start.15 = (bf16[1440,256]{1,0:T(8,128)(2,1)}, bf16[1440,256]{1,0:T(8,128)(2,1)}, u32[]{:S(2)}, u32[]{:S(2)}) collective-permute-start(bf16[1440,256]{1,0:T(8,128)(2,1)} %collective-permute-done.14.refs_18_), channel_id=1, source_target_pairs={{0,8},{1,9},{2,10},{3,11},{4,12},{5,13},{6,14},{7,15},{8,0},{9,1},... | collective-permute-start | bytes 2211848 | tf_op jit(solution)/shard_map/ppermute | solution.py:362
  161.1 22.4 %collective-permute-start.18 = (bf16[128,2048]{1,0:T(8,128)(2,1)}, bf16[128,2048]{1,0:T(8,128)(2,1)S(1)}, u32[]{:S(2)}, u32[]{:S(2)}) collective-permute-start(bf16[128,2048]{1,0:T(8,128)(2,1)} %attend.9.refs_4_), channel_id=1, source_target_pairs={{0,1},{1,0},{2,3},{3,2},{4,5},{5,4},{6,7},{7,6},{8,9},{9,8},{10,11... | collective-permute-start | bytes 1572872 | tf_op jit(solution)/shard_map/ppermute | solution.py:362
  161.5 22.0 %collective-permute-start.21 = (bf16[1440,256]{1,0:T(8,128)(2,1)}, bf16[1440,256]{1,0:T(8,128)(2,1)}, u32[]{:S(2)}, u32[]{:S(2)}) collective-permute-start(bf16[1440,256]{1,0:T(8,128)(2,1)} %collective-permute-done.12.refs_14_), channel_id=1, source_target_pairs={{0,16},{1,17},{2,18},{3,19},{4,20},{5,21},{6,22},{7,23},{8,24},{9,... | collective-permute-start | bytes 2211848 | tf_op jit(solution)/shard_map/ppermute | solution.py:362
  163.4 36.7 %collective-permute-start.20 = (bf16[1440,256]{1,0:T(8,128)(2,1)}, bf16[1440,256]{1,0:T(8,128)(2,1)}, u32[]{:S(2)}, u32[]{:S(2)}) collective-permute-start(bf16[1440,256]{1,0:T(8,128)(2,1)} %collective-permute-done.12.refs_14_), channel_id=1, source_target_pairs={{0,8},{1,9},{2,10},{3,11},{4,12},{5,13},{6,14},{7,15},{8,0},{9,1},... | collective-permute-start | bytes 2211848 | tf_op jit(solution)/shard_map/ppermute | solution.py:362
  182.6 50.2 %collective-permute-start.17 = (bf16[512,1024]{1,0:T(8,128)(2,1)}, bf16[512,1024]{1,0:T(8,128)(2,1)S(1)}, u32[]{:S(2)}, u32[]{:S(2)}) collective-permute-start(bf16[512,1024]{1,0:T(8,128)(2,1)} %attend.8.refs_1_), channel_id=1, source_target_pairs={{0,1},{1,0},{2,3},{3,2},{4,5},{5,4},{6,7},{7,6},{8,9},{9,8},{10,11... | collective-permute-start | bytes 3145736 | tf_op jit(solution)/shard_map/ppermute | solution.py:362
  183.5 18.7 %collective-permute-start.23 = (bf16[1440,256]{1,0:T(8,128)(2,1)}, bf16[1440,256]{1,0:T(8,128)(2,1)}, u32[]{:S(2)}, u32[]{:S(2)}) collective-permute-start(bf16[1440,256]{1,0:T(8,128)(2,1)} %collective-permute-done.14.refs_18_), channel_id=1, source_target_pairs={{0,16},{1,17},{2,18},{3,19},{4,20},{5,21},{6,22},{7,23},{8,24},{9,... | collective-permute-start | bytes 2211848 | tf_op jit(solution)/shard_map/ppermute | solution.py:362
  183.5 48.2 %collective-permute-start.22 = (bf16[1440,256]{1,0:T(8,128)(2,1)S(1)}, bf16[1440,256]{1,0:T(8,128)(2,1)}, u32[]{:S(2)}, u32[]{:S(2)}) collective-permute-start(bf16[1440,256]{1,0:T(8,128)(2,1)S(1)} %copy-done.7), channel_id=1, source_target_pairs={{0,6},{1,7},{2,0},{3,1},{4,2},{5,3},{6,4},{7,5},{8,14},{9,15},{10,... | collective-permute-start | bytes 2211848 | tf_op jit(solution)/shard_map/ppermute | solution.py:362
  200.1 32.7 %collective-permute-start.19 = (bf16[1440,256]{1,0:T(8,128)(2,1)S(1)}, bf16[1440,256]{1,0:T(8,128)(2,1)}, u32[]{:S(2)}, u32[]{:S(2)}) collective-permute-start(bf16[1440,256]{1,0:T(8,128)(2,1)S(1)} %copy-done.7), channel_id=1, source_target_pairs={{0,2},{1,3},{2,4},{3,5},{4,6},{5,7},{6,0},{7,1},{8,10},{9,11},{10,... | collective-permute-start | bytes 2211848 | tf_op jit(solution)/shard_map/ppermute | solution.py:362
  200.2 32.7 %collective-permute-start.24 = (bf16[1440,256]{1,0:T(8,128)(2,1)}, bf16[1440,256]{1,0:T(8,128)(2,1)}, u32[]{:S(2)}, u32[]{:S(2)}) collective-permute-start(bf16[1440,256]{1,0:T(8,128)(2,1)} %collective-permute-done.15.refs_19_), channel_id=1, source_target_pairs={{0,16},{1,17},{2,18},{3,19},{4,20},{5,21},{6,22},{7,23},{8,24},{9,... | collective-permute-start | bytes 2211848 | tf_op jit(solution)/shard_map/ppermute | solution.py:362
  252.4 3.9 %collective-permute-start.25 = (bf16[1440,512]{1,0:T(8,128)(2,1)}, bf16[1440,512]{1,0:T(8,128)(2,1)S(1)}, u32[]{:S(2)}, u32[]{:S(2)}) collective-permute-start(bf16[1440,512]{1,0:T(8,128)(2,1)} %get-tuple-element.41), channel_id=1, source_target_pairs={{0,1},{1,0},{2,3},{3,2},{4,5},{5,4},{6,7},{7,6},{8,9},{9,8},{10,11... | collective-permute-start | bytes 4423688 | tf_op jit(solution)/shard_map/ppermute | solution.py:362
  (13 other events, 220.5 us)

commit v4 on v3

--- a/solution.py
+++ b/solution.py
@@ -225,7 +225,7 @@
 def project_kernel(blocks, info, *refs):
     busy_mine, busy_got, light_mine, light_got = refs[0:2], refs[2:4], refs[4], refs[5]
     weights = refs[6 : 6 + blocks]
-    own_ref, other_ref, attended, x, w, blank, came, left = refs[6 + blocks :]
+    own_ref, other_ref, attended, x, blank, came, left = refs[6 + blocks :]
     step = pl.program_id(0)
     nodes, width = busy_mine[0].shape
     few = light_mine.shape[0]
@@ -273,9 +273,6 @@
 
         blank[...] = jnp.zeros_like(blank)
 
-    for k in range(blocks):
-        w[:, pl.ds(pl.multiple_of(info[2 + k] * depth, depth), depth)] = weights[k][...]
-
     @pl.when(step == 0)
     def _():
         for core in (0, 1):
@@ -283,7 +280,11 @@
                 copy.wait()
         for_either(lambda copy: copy.start())
 
-    done = contract_last(w[...], x[...]).astype(jnp.bfloat16)
+    part = None
+    for k in range(blocks):
+        term = contract_last(weights[k][...], x[:, pl.ds(pl.multiple_of(info[2 + k] * depth, depth), depth)])
+        part = term if part is None else part + term
+    done = part.astype(jnp.bfloat16)
     rest = jnp.zeros((done.shape[0], nodes - few), jnp.bfloat16)
 
     @pl.when(here_busy)
@@ -323,7 +324,6 @@
             ],
             scratch_shapes=[
                 pltpu.VMEM((nodes + few, total), jnp.bfloat16),
-                pltpu.VMEM((tile, total), jnp.bfloat16),
                 pltpu.VMEM((nodes - few, total), jnp.bfloat16),
                 pltpu.SemaphoreType.DMA((2, 3)),
                 pltpu.SemaphoreType.DMA((2,)),
@@ -386,7 +386,8 @@
     note = jnp.where(spot == words, node_count[0], jnp.where(spot == words + 1, cache_len[0], note))
     kv = (kc, vc, kt, vt)
     kv_got = tuple(swapped(a) for a in kv)
-    q_got = swapped(lax.dynamic_slice_in_dim(q, far * half_q, half_q, 1))
+    later_q, _ = lax.optimization_barrier((q, b0)) if plane == 4 and line == 4 else (q, b0)
+    q_got = swapped(lax.dynamic_slice_in_dim(later_q, far * half_q, half_q, 1))
     note_got = swapped(note)
     here = (q, *kv, tree_bias(words_t, tree_rows))
     there = (q_got, *kv_got, tree_bias(note_got[:words], tree_rows))
@@ -405,9 +406,8 @@
     half = node_total // BLK // 2
 
     def attend_busy(at, first, before):
-        return attend(
-            flags, here, there, sink_table, True, at, 1, first, half, node_total, tree_rows, before
-        )
+        reach = (first + half) * BLK
+        return attend(flags, here, there, sink_table, True, at, 1, first, half, node_total, reach, before)
 
     def attend_light():
         return attend(flags, here, there, sink_table, False, 0, KVH // 4, 0, 1, BLK, BLK, None)

time: 260 us -> 256 us (0.985)
  Pallas kernels: 157 us -> 149 us
    pallas_call x5, Pallas kernels: 138 us -> 131 us  [attend(): pl.pallas_call(functools.partial(attend_kernel, for_busy, len(aliases), f...]
  transfers between devices with their start and end apart: 26 -> 26, of which waited for: 4 -> 6; matrix products, arithmetic and copies ran while one was open for 2% -> 2% of each run, Pallas kernels for 54% -> 52%
where the time goes in v4:
time: 256 us; the launch traced here: 253 us
  Pallas kernels  149 us (58%)
  starting transfers between devices  50.3 us (20%)
  waiting for transfers between devices  39.9 us (16%)
  local copies, waits for them, and re-layouts  7.06 us (3%)
  other arithmetic  4.59 us (2%)
    pallas_call x5, Pallas kernels, attend(): pl.pallas_call(functools.partial(attend_kernel, for_busy, len(aliases), f...  131 us
    ppermute x26, starting transfers between devices, moved(): return lax.ppermute(x, AXES, pairs)  50.3 us
    ppermute x26, waiting for transfers between devices, moved(): return lax.ppermute(x, AXES, pairs)  39.9 us
    pallas_call x1, Pallas kernels, project(): pl.pallas_call(functools.partial(project_kernel, len(blocks)), grid_spec=...  17.1 us
  transfers between devices with their start and end apart: 26, of which 6 were waited for; matrix products, arithmetic and copies ran while one was open for 2% of the time, Pallas kernels for 52%

profile of v4, /device:TPU:9, one launch (start us, length us, event | category | flops | bytes accessed | tf_op | source)
XLA Modules:
  0.0 252.8 jit_solution(3775488837418693461)
XLA Ops:
  2.6 1.3 collective-permute-done.1
  4.2 2.1 constant_dynamic-slice_fusion
  9.2 4.5 %collective-permute-done = s32[18,512]{1,0:T(8,128)S(1)} collective-permute-done((s32[18,512]{1,0:T(8,128)S(1)}, s32[18,512]{1,0:T(8,128)S(1)}, u32[]{:S(2)}, u32[]{:S(2)}) %collective-permute-start) | collective-permute-done | bytes 36896 | tf_op jit(solution)/shard_map/ppermute | solution.py:362
  14.4 1.3 collective-permute-start.9
  15.7 1.2 collective-permute-start.8
  17.9 1.2 collective-permute-start.7
  19.7 1.4 select_convert_fusion
  21.6 1.7 compare_select_fusion.5.scal
  23.3 31.3 %attend.5.refs_13_ = bf16[512,1024]{1,0:T(8,128)(2,1)} custom-call(s32[6]{0:T(128)} %compare_select_fusion.5.scal, bf16[512,4096]{1,0:T(8,128)(2,1)} %bitcast.44, bf16[512,512]{1,0:T(8,128)(2,1)} %get-tuple-element.49.refs_1_, bf16[512,2048]{1,0:T(8,128)(2,1)} %collective-permute-done.2.refs_2_, bf16[512,512]{1,0:T(8,128)(2,1)} %get-tuple-element.48.refs_3_, ...), custom_call_target="tpu_custom_call" | custom-call | flops 5368709120 | bytes 1310720 | tf_op jit(solution)/shard_map/attend/pallas_call | solution.py:190
  55.4 1.2 collective-permute-start.13
  56.6 19.2 %attend.6.refs_0_ = bf16[512,1024]{1,0:T(8,128)(2,1)} custom-call(s32[6]{0:T(128)} %compare_select_fusion.5.scal, bf16[512,4096]{1,0:T(8,128)(2,1)} %bitcast.45, bf16[512,512]{1,0:T(8,128)(2,1)} %get-tuple-element.49.refs_1_, bf16[512,2048]{1,0:T(8,128)(2,1)} %collective-permute-done.2.refs_2_, ...), custom_call_target="tpu_custom_call", output_to_operand_aliasing={{}: (14, {})} | custom-call | flops 6442450944 | bytes 1572864 | tf_op jit(solution)/shard_map/attend/pallas_call | solution.py:190
  75.8 1.5 collective-permute-start.14
  77.4 31.3 %attend.7.refs_13_ = bf16[512,1024]{1,0:T(8,128)(2,1)} custom-call(s32[6]{0:T(128)} %compare_select_fusion.5.scal, bf16[512,4096]{1,0:T(8,128)(2,1)} %bitcast.46, bf16[512,512]{1,0:T(8,128)(2,1)} %get-tuple-element.49.refs_1_, bf16[512,2048]{1,0:T(8,128)(2,1)} %collective-permute-done.2.refs_2_, bf16[512,512]{1,0:T(8,128)(2,1)} %get-tuple-element.48.refs_3_, ...), custom_call_target="tpu_custom_call" | custom-call | flops 5368709120 | bytes 1310720 | tf_op jit(solution)/shard_map/attend/pallas_call | solution.py:190
  108.7 2.7 %collective-permute-start.16 = (bf16[512,1024]{1,0:T(8,128)(2,1)}, bf16[512,1024]{1,0:T(8,128)(2,1)S(1)}, u32[]{:S(2)}, u32[]{:S(2)}) collective-permute-start(bf16[512,1024]{1,0:T(8,128)(2,1)} %attend.6.refs_0_), channel_id=1, source_target_pairs={{0,1},{1,0},{2,3},{3,2},{4,5},{5,4},{6,7},{7,6},{8,9},{9,8},{10,11... | collective-permute-start | bytes 3145736 | tf_op jit(solution)/shard_map/ppermute | solution.py:362
  111.4 15.1 %collective-permute-start.15 = (bf16[1440,256]{1,0:T(8,128)(2,1)}, bf16[1440,256]{1,0:T(8,128)(2,1)}, u32[]{:S(2)}, u32[]{:S(2)}) collective-permute-start(bf16[1440,256]{1,0:T(8,128)(2,1)} %collective-permute-done.14.refs_18_), channel_id=1, source_target_pairs={{0,8},{1,9},{2,10},{3,11},{4,12},{5,13},{6,14},{7,15},{8,0},{9,1},... | collective-permute-start | bytes 2211848 | tf_op jit(solution)/shard_map/ppermute | solution.py:362
  126.4 30.6 %attend.9.refs_4_ = bf16[128,2048]{1,0:T(8,128)(2,1)} custom-call(s32[6]{0:T(128)} %compare_select_fusion.5.scal, bf16[512,4096]{1,0:T(8,128)(2,1)} %bitcast.47, bf16[512,512]{1,0:T(8,128)(2,1)} %get-tuple-element.49.refs_1_, bf16[512,2048]{1,0:T(8,128)(2,1)} %collective-permute-done.2.refs_2_, bf16[512,512]{1,0:T(8,128)(2,1)} %get-tuple-element.48.refs_3_, ...), custom_call_target="tpu_custom_call" | custom-call | flops 4831838208 | bytes 1179648 | tf_op jit(solution)/shard_map/attend/pallas_call | solution.py:190
  157.4 2.0 collective-permute-start.21
  159.4 19.2 %attend.8.refs_1_ = bf16[512,1024]{1,0:T(8,128)(2,1)} custom-call(s32[6]{0:T(128)} %compare_select_fusion.5.scal, bf16[512,4096]{1,0:T(8,128)(2,1)} %bitcast.48, bf16[512,512]{1,0:T(8,128)(2,1)} %get-tuple-element.49.refs_1_, bf16[512,2048]{1,0:T(8,128)(2,1)} %collective-permute-done.2.refs_2_, ...), custom_call_target="tpu_custom_call", output_to_operand_aliasing={{}: (14, {})} | custom-call | flops 6442450944 | bytes 1572864 | tf_op jit(solution)/shard_map/attend/pallas_call | solution.py:190
  179.5 17.4 %collective-permute-start.22 = (bf16[1440,256]{1,0:T(8,128)(2,1)S(1)}, bf16[1440,256]{1,0:T(8,128)(2,1)}, u32[]{:S(2)}, u32[]{:S(2)}) collective-permute-start(bf16[1440,256]{1,0:T(8,128)(2,1)S(1)} %copy-done.8), channel_id=1, source_target_pairs={{0,6},{1,7},{2,0},{3,1},{4,2},{5,3},{6,4},{7,5},{8,14},{9,15},{10,... | collective-permute-start | bytes 2211848 | tf_op jit(solution)/shard_map/ppermute | solution.py:362
  196.9 1.5 collective-permute-start.24
  198.9 29.5 %collective-permute-done.22.refs_17_ = bf16[1440,256]{1,0:T(8,128)(2,1)} collective-permute-done((bf16[1440,256]{1,0:T(8,128)(2,1)S(1)}, bf16[1440,256]{1,0:T(8,128)(2,1)}, u32[]{:S(2)}, u32[]{:S(2)}) %collective-permute-start.22) | collective-permute-done | bytes 737312 | tf_op jit(solution)/shard_map/ppermute | solution.py:362
  230.6 17.1 %project.1 = (bf16[2880,512]{1,0:T(8,128)(2,1)}, bf16[1440,512]{1,0:T(8,128)(2,1)}, bf16[512,4096]{1,0:T(8,128)(2,1)}) custom-call(s32[18]{0:T(128)} %fusion.8.info, bf16[512,1024]{1,0:T(8,128)(2,1)} %attend.6.refs_0_, bf16[512,1024]{1,0:T(8,128)(2,1)} %attend.8.refs_1_, bf16[512,1024]{1,0:T(8,128)(2,1)} %copy-done.4, bf16[512,1024]{1,0:T(8,128)(2,1)} %copy-done.5, ...), custom_call_target="tpu_custom_call" | custom-call | flops 7549747200 | bytes 11796480 | tf_op jit(solution)/shard_map/project/pallas_call | solution.py:313
  248.5 3.1 %collective-permute-done.25 = bf16[1440,512]{1,0:T(8,128)(2,1)S(1)} collective-permute-done((bf16[1440,512]{1,0:T(8,128)(2,1)}, bf16[1440,512]{1,0:T(8,128)(2,1)S(1)}, u32[]{:S(2)}, u32[]{:S(2)}) %collective-permute-start.25) | collective-permute-done | bytes 1474592 | tf_op jit(solution)/shard_map/ppermute | solution.py:362
  251.6 1.2 constant_dynamic-update-slice_fusion
  (80 shorter events, 12.1 us)
Async XLA Ops:
  6.4 17.0 %collective-permute-start.2 = (bf16[512,2048]{1,0:T(8,128)(2,1)S(1)}, bf16[512,2048]{1,0:T(8,128)(2,1)}, u32[]{:S(2)}, u32[]{:S(2)}) collective-permute-start(bf16[512,2048]{1,0:T(8,128)(2,1)S(1)} %constant_dynamic-slice_fusion), channel_id=1, source_target_pairs={{0,1},{1,0},{2,3},{3,2},{4,5},{5,4},{6,7},{7,6},{8,9},{9,8},{10,11... | collective-permute-start | bytes 6291464 | tf_op jit(solution)/shard_map/ppermute | solution.py:362
  6.8 10.2 %collective-permute-start.3 = (bf16[1024,512]{1,0:T(8,128)(2,1)S(1)}, bf16[1024,512]{1,0:T(8,128)(2,1)S(1)}, u32[]{:S(2)}, u32[]{:S(2)}) collective-permute-start(bf16[1024,512]{1,0:T(8,128)(2,1)S(1)} %bitcast.58), channel_id=1, source_target_pairs={{0,1},{1,0},{2,3},{3,2},{4,5},{5,4},{6,7},{7,6},{8,9},{9,8},{10,11... | collective-permute-start | bytes 3145736 | tf_op jit(solution)/shard_map/ppermute | solution.py:362
  6.9 16.4 %collective-permute-start.4 = (bf16[1024,512]{1,0:T(8,128)(2,1)}, bf16[1024,512]{1,0:T(8,128)(2,1)}, u32[]{:S(2)}, u32[]{:S(2)}) collective-permute-start(bf16[1024,512]{1,0:T(8,128)(2,1)} %bitcast.13.refs_5_), channel_id=1, source_target_pairs={{0,1},{1,0},{2,3},{3,2},{4,5},{5,4},{6,7},{7,6},{8,9},{9,8},{10,11... | collective-permute-start | bytes 3145736 | tf_op jit(solution)/shard_map/ppermute | solution.py:362
  8.7 5.0 %collective-permute-start = (s32[18,512]{1,0:T(8,128)S(1)}, s32[18,512]{1,0:T(8,128)S(1)}, u32[]{:S(2)}, u32[]{:S(2)}) collective-permute-start(s32[18,512]{1,0:T(8,128)S(1)} %select_select_fusion), channel_id=1, source_target_pairs={{0,1},{1,0},{2,3},{3,2},{4,5},{5,4},{6,7},{7,6},{8,9},{9,8},{10,11... | collective-permute-start | bytes 110600 | tf_op jit(solution)/shard_map/ppermute | solution.py:362
  8.9 5.5 %collective-permute-start.5 = (bf16[512,512]{1,0:T(8,128)(2,1)S(1)}, bf16[512,512]{1,0:T(8,128)(2,1)S(1)}, u32[]{:S(2)}, u32[]{:S(2)}) collective-permute-start(bf16[512,512]{1,0:T(8,128)(2,1)S(1)} %bitcast.64), channel_id=1, source_target_pairs={{0,1},{1,0},{2,3},{3,2},{4,5},{5,4},{6,7},{7,6},{8,9},{9,8},{10,11... | collective-permute-start | bytes 1572872 | tf_op jit(solution)/shard_map/ppermute | solution.py:362
  14.4 40.3 %collective-permute-start.9 = (bf16[1440,256]{1,0:T(8,128)(2,1)S(1)}, bf16[1440,256]{1,0:T(8,128)(2,1)}, u32[]{:S(2)}, u32[]{:S(2)}) collective-permute-start(bf16[1440,256]{1,0:T(8,128)(2,1)S(1)} %maximum_select_fusion.refs_6_), channel_id=1, source_target_pairs={{0,2},{1,3},{2,4},{3,5},{4,6},{5,7},{6,0},{7,1},{8,10},{9,11},{10,... | collective-permute-start | bytes 2211848 | tf_op jit(solution)/shard_map/ppermute | solution.py:362
  15.7 39.0 %collective-permute-start.8 = (bf16[1440,256]{1,0:T(8,128)(2,1)S(1)}, bf16[1440,256]{1,0:T(8,128)(2,1)}, u32[]{:S(2)}, u32[]{:S(2)}) collective-permute-start(bf16[1440,256]{1,0:T(8,128)(2,1)S(1)} %maximum_select_fusion.refs_6_), channel_id=1, source_target_pairs={{0,16},{1,17},{2,18},{3,19},{4,20},{5,21},{6,22},{7,23},{8,24},{9,... | collective-permute-start | bytes 2211848 | tf_op jit(solution)/shard_map/ppermute | solution.py:362
  17.9 36.8 %collective-permute-start.7 = (bf16[1440,256]{1,0:T(8,128)(2,1)S(1)}, bf16[1440,256]{1,0:T(8,128)(2,1)}, u32[]{:S(2)}, u32[]{:S(2)}) collective-permute-start(bf16[1440,256]{1,0:T(8,128)(2,1)S(1)} %maximum_select_fusion.refs_6_), channel_id=1, source_target_pairs={{0,8},{1,9},{2,10},{3,11},{4,12},{5,13},{6,14},{7,15},{8,0},{9,1},... | collective-permute-start | bytes 2211848 | tf_op jit(solution)/shard_map/ppermute | solution.py:362
  54.7 21.1 %collective-permute-start.10 = (bf16[1440,256]{1,0:T(8,128)(2,1)}, bf16[1440,256]{1,0:T(8,128)(2,1)S(1)}, u32[]{:S(2)}, u32[]{:S(2)}) collective-permute-start(bf16[1440,256]{1,0:T(8,128)(2,1)} %collective-permute-done.8.refs_8_), channel_id=1, source_target_pairs={{0,8},{1,9},{2,10},{3,11},{4,12},{5,13},{6,14},{7,15},{8,0},{9,1},... | collective-permute-start | bytes 2211848 | tf_op jit(solution)/shard_map/ppermute | solution.py:362
  55.0 20.8 %collective-permute-start.12 = (bf16[1440,256]{1,0:T(8,128)(2,1)S(1)}, bf16[1440,256]{1,0:T(8,128)(2,1)}, u32[]{:S(2)}, u32[]{:S(2)}) collective-permute-start(bf16[1440,256]{1,0:T(8,128)(2,1)S(1)} %maximum_select_fusion.refs_6_), channel_id=1, source_target_pairs={{0,6},{1,7},{2,0},{3,1},{4,2},{5,3},{6,4},{7,5},{8,14},{9,15},{10,... | collective-permute-start | bytes 2211848 | tf_op jit(solution)/shard_map/ppermute | solution.py:362
  55.2 20.7 %collective-permute-start.11 = (bf16[1440,256]{1,0:T(8,128)(2,1)}, bf16[1440,256]{1,0:T(8,128)(2,1)S(1)}, u32[]{:S(2)}, u32[]{:S(2)}) collective-permute-start(bf16[1440,256]{1,0:T(8,128)(2,1)} %collective-permute-done.9.refs_10_), channel_id=1, source_target_pairs={{0,16},{1,17},{2,18},{3,19},{4,20},{5,21},{6,22},{7,23},{8,24},{9,... | collective-permute-start | bytes 2211848 | tf_op jit(solution)/shard_map/ppermute | solution.py:362
  55.4 56.0 %collective-permute-start.13 = (bf16[1440,256]{1,0:T(8,128)(2,1)}, bf16[1440,256]{1,0:T(8,128)(2,1)S(1)}, u32[]{:S(2)}, u32[]{:S(2)}) collective-permute-start(bf16[1440,256]{1,0:T(8,128)(2,1)} %collective-permute-done.9.refs_10_), channel_id=1, source_target_pairs={{0,8},{1,9},{2,10},{3,11},{4,12},{5,13},{6,14},{7,15},{8,0},{9,1},... | collective-permute-start | bytes 2211848 | tf_op jit(solution)/shard_map/ppermute | solution.py:362
  75.8 35.5 %collective-permute-start.14 = (bf16[1440,256]{1,0:T(8,128)(2,1)}, bf16[1440,256]{1,0:T(8,128)(2,1)}, u32[]{:S(2)}, u32[]{:S(2)}) collective-permute-start(bf16[1440,256]{1,0:T(8,128)(2,1)} %collective-permute-done.9.refs_10_), channel_id=1, source_target_pairs={{0,2},{1,3},{2,4},{3,5},{4,6},{5,7},{6,0},{7,1},{8,10},{9,11},{10,... | collective-permute-start | bytes 2211848 | tf_op jit(solution)/shard_map/ppermute | solution.py:362
  108.7 88.2 %collective-permute-start.16 = (bf16[512,1024]{1,0:T(8,128)(2,1)}, bf16[512,1024]{1,0:T(8,128)(2,1)S(1)}, u32[]{:S(2)}, u32[]{:S(2)}) collective-permute-start(bf16[512,1024]{1,0:T(8,128)(2,1)} %attend.6.refs_0_), channel_id=1, source_target_pairs={{0,1},{1,0},{2,3},{3,2},{4,5},{5,4},{6,7},{7,6},{8,9},{9,8},{10,11... | collective-permute-start | bytes 3145736 | tf_op jit(solution)/shard_map/ppermute | solution.py:362
  111.4 67.2 %collective-permute-start.15 = (bf16[1440,256]{1,0:T(8,128)(2,1)}, bf16[1440,256]{1,0:T(8,128)(2,1)}, u32[]{:S(2)}, u32[]{:S(2)}) collective-permute-start(bf16[1440,256]{1,0:T(8,128)(2,1)} %collective-permute-done.14.refs_18_), channel_id=1, source_target_pairs={{0,8},{1,9},{2,10},{3,11},{4,12},{5,13},{6,14},{7,15},{8,0},{9,1},... | collective-permute-start | bytes 2211848 | tf_op jit(solution)/shard_map/ppermute | solution.py:362
  157.0 22.4 %collective-permute-start.18 = (bf16[128,2048]{1,0:T(8,128)(2,1)}, bf16[128,2048]{1,0:T(8,128)(2,1)S(1)}, u32[]{:S(2)}, u32[]{:S(2)}) collective-permute-start(bf16[128,2048]{1,0:T(8,128)(2,1)} %attend.9.refs_4_), channel_id=1, source_target_pairs={{0,1},{1,0},{2,3},{3,2},{4,5},{5,4},{6,7},{7,6},{8,9},{9,8},{10,11... | collective-permute-start | bytes 1572872 | tf_op jit(solution)/shard_map/ppermute | solution.py:362
  157.4 22.0 %collective-permute-start.21 = (bf16[1440,256]{1,0:T(8,128)(2,1)}, bf16[1440,256]{1,0:T(8,128)(2,1)}, u32[]{:S(2)}, u32[]{:S(2)}) collective-permute-start(bf16[1440,256]{1,0:T(8,128)(2,1)} %collective-permute-done.12.refs_14_), channel_id=1, source_target_pairs={{0,16},{1,17},{2,18},{3,19},{4,20},{5,21},{6,22},{7,23},{8,24},{9,... | collective-permute-start | bytes 2211848 | tf_op jit(solution)/shard_map/ppermute | solution.py:362
  159.4 37.5 %collective-permute-start.20 = (bf16[1440,256]{1,0:T(8,128)(2,1)}, bf16[1440,256]{1,0:T(8,128)(2,1)}, u32[]{:S(2)}, u32[]{:S(2)}) collective-permute-start(bf16[1440,256]{1,0:T(8,128)(2,1)} %collective-permute-done.12.refs_14_), channel_id=1, source_target_pairs={{0,8},{1,9},{2,10},{3,11},{4,12},{5,13},{6,14},{7,15},{8,0},{9,1},... | collective-permute-start | bytes 2211848 | tf_op jit(solution)/shard_map/ppermute | solution.py:362
  178.6 51.0 %collective-permute-start.17 = (bf16[512,1024]{1,0:T(8,128)(2,1)}, bf16[512,1024]{1,0:T(8,128)(2,1)S(1)}, u32[]{:S(2)}, u32[]{:S(2)}) collective-permute-start(bf16[512,1024]{1,0:T(8,128)(2,1)} %attend.8.refs_1_), channel_id=1, source_target_pairs={{0,1},{1,0},{2,3},{3,2},{4,5},{5,4},{6,7},{7,6},{8,9},{9,8},{10,11... | collective-permute-start | bytes 3145736 | tf_op jit(solution)/shard_map/ppermute | solution.py:362
  179.4 19.5 %collective-permute-start.23 = (bf16[1440,256]{1,0:T(8,128)(2,1)}, bf16[1440,256]{1,0:T(8,128)(2,1)}, u32[]{:S(2)}, u32[]{:S(2)}) collective-permute-start(bf16[1440,256]{1,0:T(8,128)(2,1)} %collective-permute-done.14.refs_18_), channel_id=1, source_target_pairs={{0,16},{1,17},{2,18},{3,19},{4,20},{5,21},{6,22},{7,23},{8,24},{9,... | collective-permute-start | bytes 2211848 | tf_op jit(solution)/shard_map/ppermute | solution.py:362
  179.5 48.9 %collective-permute-start.22 = (bf16[1440,256]{1,0:T(8,128)(2,1)S(1)}, bf16[1440,256]{1,0:T(8,128)(2,1)}, u32[]{:S(2)}, u32[]{:S(2)}) collective-permute-start(bf16[1440,256]{1,0:T(8,128)(2,1)S(1)} %copy-done.8), channel_id=1, source_target_pairs={{0,6},{1,7},{2,0},{3,1},{4,2},{5,3},{6,4},{7,5},{8,14},{9,15},{10,... | collective-permute-start | bytes 2211848 | tf_op jit(solution)/shard_map/ppermute | solution.py:362
  196.9 32.7 %collective-permute-start.19 = (bf16[1440,256]{1,0:T(8,128)(2,1)S(1)}, bf16[1440,256]{1,0:T(8,128)(2,1)}, u32[]{:S(2)}, u32[]{:S(2)}) collective-permute-start(bf16[1440,256]{1,0:T(8,128)(2,1)S(1)} %copy-done.8), channel_id=1, source_target_pairs={{0,2},{1,3},{2,4},{3,5},{4,6},{5,7},{6,0},{7,1},{8,10},{9,11},{10,... | collective-permute-start | bytes 2211848 | tf_op jit(solution)/shard_map/ppermute | solution.py:362
  196.9 32.7 %collective-permute-start.24 = (bf16[1440,256]{1,0:T(8,128)(2,1)}, bf16[1440,256]{1,0:T(8,128)(2,1)}, u32[]{:S(2)}, u32[]{:S(2)}) collective-permute-start(bf16[1440,256]{1,0:T(8,128)(2,1)} %collective-permute-done.15.refs_19_), channel_id=1, source_target_pairs={{0,16},{1,17},{2,18},{3,19},{4,20},{5,21},{6,22},{7,23},{8,24},{9,... | collective-permute-start | bytes 2211848 | tf_op jit(solution)/shard_map/ppermute | solution.py:362
  247.7 3.8 %collective-permute-start.25 = (bf16[1440,512]{1,0:T(8,128)(2,1)}, bf16[1440,512]{1,0:T(8,128)(2,1)S(1)}, u32[]{:S(2)}, u32[]{:S(2)}) collective-permute-start(bf16[1440,512]{1,0:T(8,128)(2,1)} %get-tuple-element.43), channel_id=1, source_target_pairs={{0,1},{1,0},{2,3},{3,2},{4,5},{5,4},{6,7},{7,6},{8,9},{9,8},{10,11... | collective-permute-start | bytes 4423688 | tf_op jit(solution)/shard_map/ppermute | solution.py:362
  (18 other events, 254.5 us)
